TPU v7x, 256 devices: a whole 4x4x8 slice. The times are simulated.
256 devices in a mesh: dp: 32 (over z, x), fsdp: 8 (over y, core).
Axes of the slice: x: 4, y: 4, z: 8, core: 2. Of those that a mesh axis runs over, the one named last changes fastest.
Arguments:
- latents: bfloat16 [384, 2, 4096], P('dp'), may hold values from -6 to 6
- noise: bfloat16 [384, 2, 4096], P('dp'), may hold values from -6 to 6
- behavior_velocity: bfloat16 [384, 2, 4096], P('dp'), may hold values from -6 to 6
- timestep: int32 [384, 2], P('dp'), may hold values from 0 to 9
- reward_rank_integer: int32 [384], P('dp'), may hold values from 0 to 1023
- surviving_source_index: int32 [192], replicated, may hold values from 0 to 31, as said below
- surviving_slot_index: int32 [192], replicated, may hold values from 0 to 11, as said below
- group_kept_count: int32 [48], replicated, may hold values from 1 to 24, 192 in all
- patch_input_weight: bfloat16 [64, 1536], replicated, may hold values from -0.75 to 0.75
- modulation_lookup: float32 [10, 3, 1536], replicated, may hold values from -3 to 3
- up_projection_weight: bfloat16 [1536, 8192], P(None, 'fsdp'), may hold values from -0.15625 to 0.15625
- down_projection_weight: bfloat16 [1536, 8192], P(None, 'fsdp'), may hold values from -0.0625 to 0.0625
- velocity_head_weight: bfloat16 [1536, 64], replicated, may hold values from -0.15625 to 0.15625
Outputs:
- up_weight_gradient: float32 [1536, 8192], P('dp', 'fsdp')
- down_weight_gradient: float32 [1536, 8192], P('dp', 'fsdp')
- loss: float32 [], replicated
Inputs may be any that keep to these rules, and one draw needn't show every extreme that they name: `surviving_source_index`: survivors are listed by source in ascending order; survivor j is trained on dp index j // 6, and every survivor of source d is trained on dp index d or d + 1. `surviving_slot_index`: the slots of one source's survivors are distinct.
All inputs are finite; a program needn't handle non-finite values.
Results may differ from a plain program's by a relative error of at most 0.013.
Values may be sent and summed in bfloat16 or wider, within the bound.
A program may use at most 128 MiB of HBM per device.

v0:
```python
import jax
import jax.numpy as jnp
from jax import lax
from jax.sharding import Mesh
from jax.sharding import PartitionSpec as P

KSTEPS = 10
DP = ("dp_0", "dp_1")


clip_range = 0.2
noise_level = 0.7
norm_eps = 1e-06


def shortened(x):

    def short(part):
        return part.astype(jnp.bfloat16) if part.dtype == jnp.float32 else part

    return jax.tree.map(short, x)


def shifted(value, axis, steps):
    count = lax.axis_size(axis)
    initial, last = (max(0, -steps), min(count, count - steps))
    return lax.ppermute(value, axis, [(source, source + steps) for source in range(initial, last)])


def sent_to_all(x, axis):
    count = lax.axis_size(axis)
    return lax.all_to_all(jnp.broadcast_to(x[None], (count, *x.shape)), axis, 0, 0, tiled=True)


def taken_together(x, axis):
    everything = sent_to_all(x, axis)
    return jnp.sum(everything, axis=0)


def in_order(parts, dim):
    lengths = list(parts.shape[1:])
    lengths[dim] *= parts.shape[0]
    return jnp.moveaxis(parts, 0, dim).reshape(lengths)


def collect(x, axis, dim):
    return in_order(sent_to_all(x, axis), dim)


def own_rows_2(terms, axes):
    total = terms.astype(jnp.bfloat16)
    for axis in axes:
        total = lax.psum_scatter(total, axis, scatter_dimension=0, tiled=True)
    return total.astype(jnp.float32)


def step_ratio(indices, count):
    spacing = 1.0 / count
    level = 1.0 - indices.astype(jnp.float32) * spacing
    return jnp.sqrt(spacing * (1.0 - level + spacing) / level) / noise_level


def layer_norm(values):
    center = values - jnp.mean(values, axis=-1, keepdims=True)
    variance = jnp.mean(center * center, axis=-1, keepdims=True)
    inverse = lax.rsqrt(variance + norm_eps)
    return (center * inverse, inverse)


def smooth_gate(values):
    return jax.nn.gelu(values, approximate=True)


def membership_matrix(surviving_identifiers, kept_mask):
    group_ends = jnp.cumsum(kept_mask)
    group_starts = group_ends - kept_mask
    inside_clip_mask = (surviving_identifiers[:, None] >= group_starts[None, :]) & (
        surviving_identifiers[:, None] < group_ends[None, :]
    )
    return inside_clip_mask.astype(jnp.int32)


def advantages(ranks, member_mask, kept_mask, sums):
    count = jnp.sum(member_mask * kept_mask[None, :], axis=1)
    first = jnp.sum(member_mask * sums[0][None, :], axis=1)
    second = jnp.sum(member_mask * sums[1][None, :], axis=1)
    spread = (count * second - first * first).astype(jnp.float32)
    counts = count.astype(jnp.float32)
    deviation = jnp.sqrt(spread) / counts
    return (ranks.astype(jnp.float32) - first.astype(jnp.float32) / counts) / jnp.maximum(
        deviation, 1.0
    )


def shards(
    latents,
    noise,
    behavior_velocity,
    timestep,
    reward_rank_integer,
    surviving_source_index,
    surviving_slot_index,
    group_kept_count,
    patch_input_weight,
    modulation_lookup,
    up_projection_weight,
    down_projection_weight,
    velocity_head_weight,
):
    owner = lax.axis_index(DP)
    owner_ranks = lax.axis_size(DP)
    surviving_count = surviving_source_index.shape[0]
    trajectory_rows = surviving_count // owner_ranks
    leading_identifier = owner * trajectory_rows
    owned_source_index = lax.dynamic_slice_in_dim(
        surviving_source_index, leading_identifier, trajectory_rows
    )
    owned_slot_index = lax.dynamic_slice_in_dim(
        surviving_slot_index, leading_identifier, trajectory_rows
    )
    local_data = (latents, noise, behavior_velocity, timestep, reward_rank_integer)

    def selection_mask(slot_list):
        return tuple((jnp.take(array, slot_list, axis=0) for array in local_data))

    own_rows = selection_mask(owned_slot_index)
    following_leader = jnp.minimum(owner + 1, owner_ranks - 1) * trajectory_rows
    outgoing_rows = selection_mask(
        lax.dynamic_slice_in_dim(surviving_slot_index, following_leader, trajectory_rows)
    )
    arrived = jax.tree.map(
        lambda part, own: part.astype(own.dtype),
        shifted(shortened(outgoing_rows), DP, 1),
        outgoing_rows,
    )
    from_left = owned_source_index != owner
    gathered = tuple(
        (
            jnp.where(from_left.reshape((trajectory_rows,) + (1,) * (mine.ndim - 1)), came, mine)
            for mine, came in zip(own_rows, arrived)
        )
    )
    samples, noises, olds, stamps, ranks = gathered
    member_mask = membership_matrix(
        leading_identifier + jnp.arange(trajectory_rows, dtype=jnp.int32), group_kept_count
    )
    partial_value = jnp.stack(
        [
            jnp.sum(member_mask * ranks[:, None], axis=0),
            jnp.sum(member_mask * (ranks * ranks)[:, None], axis=0),
        ]
    ).astype(jnp.int32)
    totals = taken_together(partial_value, DP)
    advantage = advantages(ranks, member_mask, group_kept_count, totals)
    patch = patch_input_weight.shape[0]
    width = patch_input_weight.shape[1]
    hidden_shard = up_projection_weight.shape[1]
    step_indices = stamps.shape[1]
    units = trajectory_rows * step_indices
    seq = samples.shape[2] // patch
    rows = units * seq
    stamp_flat = stamps.reshape(units)
    modulation = jnp.take(modulation_lookup, stamp_flat, axis=0)
    embedded = jnp.dot(
        samples.reshape(rows, patch), patch_input_weight, preferred_element_type=jnp.float32
    ).reshape(units, seq, width)
    normed, unused_value = layer_norm(embedded)
    modulated = (
        (normed * (1.0 + modulation[:, 1][:, None]) + modulation[:, 0][:, None])
        .astype(jnp.bfloat16)
        .reshape(rows, width)
    )
    pre = jnp.dot(modulated, up_projection_weight, preferred_element_type=jnp.float32)
    activated = smooth_gate(pre).astype(jnp.bfloat16)
    projected = lax.dot_general(
        activated,
        down_projection_weight,
        (((1,), (1,)), ((), ())),
        preferred_element_type=jnp.float32,
    )
    per_unit_gain = jnp.repeat(advantage, step_indices)
    coeff = step_ratio(stamp_flat, KSTEPS)
    gates = modulation[:, 2]
    embedded_rows = embedded.reshape(rows, width)
    old_rows = olds.reshape(rows, patch)
    noise_rows = noises.reshape(rows, patch)

    def head_terms(summed, lower, count):
        row_ids = lower + jnp.arange(count, dtype=jnp.int32)
        owner_unit = row_ids // seq
        gate_rows = jnp.take(gates, owner_unit, axis=0)
        mixed = lax.dynamic_slice_in_dim(embedded_rows, lower, count) + gate_rows * summed
        final, inverse = layer_norm(mixed)
        velocity = jnp.dot(
            final.astype(jnp.bfloat16), velocity_head_weight, preferred_element_type=jnp.float32
        )
        target = lax.dynamic_slice_in_dim(old_rows, lower, count).astype(jnp.float32)
        drawn = lax.dynamic_slice_in_dim(noise_rows, lower, count).astype(jnp.float32)
        coeff_rows = jnp.take(coeff, owner_unit)[:, None]
        error = velocity - target
        terms = coeff_rows * drawn * error + 0.5 * coeff_rows * coeff_rows * error * error
        unit_member = (owner_unit[:, None] == jnp.arange(units, dtype=jnp.int32)[None, :]).astype(
            jnp.float32
        )
        unit_sums = jnp.sum(unit_member * jnp.sum(terms, axis=1)[:, None], axis=0)

        def backward(loss_slope):
            slope_rows = jnp.take(loss_slope, owner_unit)[:, None]
            dvelocity = (
                slope_rows
                * (-(coeff_rows * drawn + coeff_rows * coeff_rows * error) / (seq * patch))
            ).astype(jnp.bfloat16)
            dfinal = lax.dot_general(
                dvelocity,
                velocity_head_weight,
                (((1,), (1,)), ((), ())),
                preferred_element_type=jnp.float32,
            )
            dmixed = inverse * (
                dfinal
                - jnp.mean(dfinal, axis=-1, keepdims=True)
                - final * jnp.mean(dfinal * final, axis=-1, keepdims=True)
            )
            return (gate_rows * dmixed).astype(jnp.bfloat16)

        return (unit_sums, backward)

    share = rows // lax.axis_size("fsdp")
    lower = lax.axis_index("fsdp") * share
    summed = lax.psum_scatter(projected, "fsdp", scatter_dimension=0, tiled=True)
    part_sums, backward = head_terms(summed, lower, share)
    unit_sums = taken_together(part_sums, "fsdp")
    logratio = -unit_sums / (seq * patch)
    likelihood_ratio = jnp.exp(logratio)
    clipped = jnp.clip(likelihood_ratio, 1.0 - clip_range, 1.0 + clip_range)
    plain = likelihood_ratio * per_unit_gain
    bounded = clipped * per_unit_gain
    unit_loss = -jnp.minimum(plain, bounded)
    live_mask = (plain <= bounded).astype(jnp.float32)
    loss_slope = -per_unit_gain * likelihood_ratio * live_mask / (surviving_count * step_indices)
    replica_loss, loss_slope = (jnp.sum(unit_loss), loss_slope)
    upstream = collect(backward(loss_slope), "fsdp", 0)
    total_count = taken_together(replica_loss, DP) / (surviving_count * step_indices)
    dactivated = jnp.dot(upstream, down_projection_weight, preferred_element_type=jnp.float32)
    unused_value, pull = jax.vjp(smooth_gate, pre)
    dpre = pull(dactivated)[0].astype(jnp.bfloat16)
    contract = (((0,), (0,)), ((), ()))
    grads = own_rows_2(
        jnp.concatenate(
            [
                lax.dot_general(modulated, dpre, contract, preferred_element_type=jnp.float32),
                lax.dot_general(upstream, activated, contract, preferred_element_type=jnp.float32),
            ],
            axis=1,
        ),
        DP,
    )
    return (grads[:, :hidden_shard], grads[:, hidden_shard:], total_count)


def solution(mesh):
    finer = Mesh(mesh.devices.reshape(8, 4, mesh.shape["fsdp"]), ("dp_0", "dp_1", "fsdp"))
    in_specs = (
        P(DP, None, None),
        P(DP, None, None),
        P(DP, None, None),
        P(DP, None),
        P(DP),
        P(),
        P(),
        P(),
        P(),
        P(),
        P(None, "fsdp"),
        P(None, "fsdp"),
        P(),
    )
    out_specs = (P(DP, "fsdp"), P(DP, "fsdp"), P())
    return jax.shard_map(
        shards, mesh=finer, in_specs=in_specs, out_specs=out_specs, check_vma=False
    )
```

profile of v0, /device:TPU:32, one launch (start us, length us, event | category | flops | bytes accessed | tf_op | source)
XLA Modules:
  0.0 304.1 jit_solution(17713014593073793346)
XLA Ops:
  9.5 3.4 %collective-permute-start.4 = (s32[6]{0:T(128)S(1)}, s32[6]{0:T(128)S(1)}, u32[]{:S(2)}, u32[]{:S(2)}) collective-permute-start(s32[6]{0:T(128)S(1)} %broadcast_select_fusion.11), channel_id=1, source_target_pairs={{0,8},{8,16},{16,24},{24,32},{32,40},{40,48},{48,56},{56,64},{64,7... | collective-permute-start | bytes 80 | tf_op jit(solution)/shard_map/ppermute | solution.py:27
  18.9 3.4 %collective-permute-start = (bf16[6,2,4096]{2,1,0:T(2,128)(2,1)}, bf16[6,2,4096]{2,1,0:T(2,128)(2,1)}, u32[]{:S(2)}, u32[]{:S(2)}) collective-permute-start(bf16[6,2,4096]{2,1,0:T(2,128)(2,1)} %get-tuple-element.80), channel_id=1, source_target_pairs={{0,8},{8,16},{16,24},{24,32},{32,40},{40,48},{48,56},{56,64},{64,7... | collective-permute-start | bytes 294920 | tf_op jit(solution)/shard_map/ppermute | solution.py:27
  22.3 3.1 %collective-permute-start.2 = (bf16[6,2,4096]{2,1,0:T(2,128)(2,1)}, bf16[6,2,4096]{2,1,0:T(2,128)(2,1)}, u32[]{:S(2)}, u32[]{:S(2)}) collective-permute-start(bf16[6,2,4096]{2,1,0:T(2,128)(2,1)} %get-tuple-element.79), channel_id=1, source_target_pairs={{0,8},{8,16},{16,24},{24,32},{32,40},{40,48},{48,56},{56,64},{64,7... | collective-permute-start | bytes 294920 | tf_op jit(solution)/shard_map/ppermute | solution.py:27
  25.4 3.7 %collective-permute-start.3 = (bf16[6,2,4096]{2,1,0:T(2,128)(2,1)}, bf16[6,2,4096]{2,1,0:T(2,128)(2,1)}, u32[]{:S(2)}, u32[]{:S(2)}) collective-permute-start(bf16[6,2,4096]{2,1,0:T(2,128)(2,1)} %get-tuple-element.78), channel_id=1, source_target_pairs={{0,8},{8,16},{16,24},{24,32},{32,40},{40,48},{48,56},{56,64},{64,7... | collective-permute-start | bytes 294920 | tf_op jit(solution)/shard_map/ppermute | solution.py:27
  30.6 3.4 %collective-permute-start.1 = (s32[6,2]{1,0:T(8,128)S(1)}, s32[6,2]{1,0:T(8,128)S(1)}, u32[]{:S(2)}, u32[]{:S(2)}) collective-permute-start(s32[6,2]{1,0:T(8,128)S(1)} %broadcast_select_fusion.10), channel_id=1, source_target_pairs={{0,8},{8,16},{16,24},{24,32},{32,40},{40,48},{48,56},{56,64},{64,7... | collective-permute-start | bytes 152 | tf_op jit(solution)/shard_map/ppermute | solution.py:27
  35.3 2.3 gather_fusion.3
  37.6 2.3 gather_fusion.7
  39.9 2.3 gather_fusion.9
  46.5 2.2 broadcast_select_fusion
  49.8 1.7 fusion.40
  55.2 2.6 fusion.41
  59.4 5.6 %fusion.30 = f32[768,1536]{1,0:T(8,128)} fusion(bf16[1536,1024]{1,0:T(8,128)(2,1)S(1)} %copy-done, f32[768,1024]{1,0:T(8,128)S(1)} %fusion.41), kind=kOutput, calls=%fused_computation.150 | convolution fusion | flops 2422996992 | bytes 11010048 | tf_op jit(solution)/shard_map/dot_general | solution.py:175
  67.8 10.1 %all-to-all-start.1 = ((s32[32,2,48]{2,1,0:T(2,128)}), s32[32,2,48]{2,1,0:T(2,128)}, u32[]{:S(2)}, u32[]{:S(2)}) async-start(s32[32,2,48]{2,1,0:T(2,128)} %broadcast_in_dim.118), calls=%async_computation.2 | async-start | bytes 65536 | tf_op jit(solution)/shard_map/all_to_all | solution.py:32
  78.6 7.9 %fusion.32 = (f32[96]{0:T(128)}, f32[96]{0:T(128)S(1)}) fusion(f32[]{:T(128)} %bitcast.15, f32[]{:T(128)} %bitcast.14, f32[]{:T(128)} %bitcast.13, f32[]{:T(128)} %bitcast.12, f32[]{:T(128)} %bitcast.11, f32[]{:T(128)} %bitcast.10, f32[]{:T(128)} %bitcast.9, f32[]{:T(128)} %bitcast.8, f32[]{:T(128)} %bitcast.7, f32[]{:T(128)} %bitcast.6, f32[]{:T(128)} %bitcast.5, ...), kind=kLoop, calls=%fused_computation.152 | loop fusion | flops 4416 | bytes 820 | tf_op jit(solution)/shard_map/mul | solution.py:211
  93.6 14.9 %reduce-scatter.8.cloned.1.call-done = f32[96,1536]{1,0:T(8,128)} async-done(((f32[768,1536]{1,0:T(8,128)}), f32[96,1536]{1,0:T(8,128)}) %reduce-scatter.8.cloned.1.call-update) | async-done | bytes 589840 | tf_op jit(solution)/shard_map/reduce_scatter | solution.py:230
  108.5 1.7 fusion.35
  113.3 3.3 %all-to-all-start = ((f32[8,1,12]{2,1,0:T(1,128)}), f32[8,1,12]{2,1,0:T(1,128)S(1)}, u32[]{:S(2)}, u32[]{:S(2)}) async-start(f32[8,1,12]{2,1,0:T(1,128)} %broadcast_in_dim.117), calls=%async_computation.1 | async-start | bytes 8192 | tf_op jit(solution)/shard_map/all_to_all | solution.py:32
  117.1 4.7 %all-to-all-done = f32[8,1,12]{2,1,0:T(1,128)S(1)} async-done(((f32[8,1,12]{2,1,0:T(1,128)}), f32[8,1,12]{2,1,0:T(1,128)S(1)}, u32[]{:S(2)}, u32[]{:S(2)}) %all-to-all-start) | async-done | bytes 416 | tf_op jit(solution)/shard_map/all_to_all | solution.py:32
  123.1 7.4 %fusion.23 = f32[96]{0:T(128)S(1)} fusion(f32[]{:T(128)} %bitcast.33, f32[]{:T(128)} %bitcast.32, f32[]{:T(128)} %bitcast.31, f32[]{:T(128)} %bitcast.30, f32[]{:T(128)} %bitcast.29, f32[]{:T(128)} %bitcast.28, f32[]{:T(128)} %bitcast.27, f32[]{:T(128)} %bitcast.26, f32[]{:T(128)} %bitcast.25, f32[]{:T(128)} %bitcast.24, f32[]{:T(128)} %bitcast.23, ...), kind=kLoop, calls=%fused_computation.139 | loop fusion | flops 4416 | bytes 436 | tf_op jit(solution)/shard_map/mul | solution.py:210
  133.8 32.5 %all_to_all.22 = bf16[8,96,1536]{2,1,0:T(8,128)(2,1)S(1)} all-to-all(bf16[8,96,1536]{2,1,0:T(8,128)(2,1)S(1)} %broadcast_in_dim.120), channel_id=1, replica_groups=mesh['dp_0'=8,'dp_1'=4,'fsdp'=8] {'fsdp'}, dimensions={0} | all-to-all | bytes 4718592 | tf_op jit(solution)/shard_map/all_to_all | solution.py:32
  166.3 2.6 fusion.42
  168.9 3.1 %convolution_convert_fusion = bf16[1536,1024]{0,1:T(8,128)(2,1)S(1)} fusion(bf16[768,1536]{1,0:T(8,128)(2,1)S(1)} %bitcast.67, f32[768,1024]{1,0:T(8,128)S(1)} %copy-done.18), kind=kOutput, calls=%fused_computation.19 | convolution fusion | flops 2424569856 | bytes 8650752 | tf_op jit(solution)/shard_map/dot_general | solution.py:252
  172.0 4.1 %convolution_convert_fusion.1 = bf16[1536,1024]{0,1:T(8,128)(2,1)S(1)} fusion(bf16[768,1536]{1,0:T(8,128)(2,1)S(1)} %copy-done.4, f32[768,1024]{1,0:T(8,128)S(1)} %copy-done.18, f32[768,1024]{1,0:T(8,128)S(1)} %fusion.42), kind=kOutput, calls=%fused_computation.20 | convolution fusion | flops 2433220608 | bytes 11796480 | tf_op jit(solution)/shard_map/dot_general | solution.py:251
  176.1 3.1 %pad_maximum_fusion = bf16[1536,2048]{0,1:T(8,128)(2,1)} fusion(bf16[1536,1024]{0,1:T(8,128)(2,1)S(1)} %convolution_convert_fusion, bf16[1536,1024]{0,1:T(8,128)(2,1)S(1)} %convolution_convert_fusion.1), kind=kLoop, calls=%fused_computation.12 | loop fusion | flops 12582912 | bytes 12582912 | tf_op jit(solution)/shard_map/concatenate | solution.py:249
  179.2 8.7 %copy.52 = bf16[1536,2048]{1,0:T(8,128)(2,1)} copy(bf16[1536,2048]{0,1:T(8,128)(2,1)} %pad_maximum_fusion) | data formatting | bytes 12582912
  187.9 72.6 %reduce-scatter.10.cloned.1.call-done = bf16[192,2048]{1,0:T(8,128)(2,1)} async-done(((bf16[1536,2048]{1,0:T(8,128)(2,1)}), bf16[192,2048]{1,0:T(8,128)(2,1)}) %reduce-scatter.10.cloned.1.call-update) | async-done | bytes 786448
  261.2 17.5 %all_to_all.23 = f32[32,1,1]{2,1,0:T(1,128)S(1)} all-to-all(f32[32,1,1]{2,1,0:T(1,128)S(1)} %broadcast_in_dim.121), channel_id=1, replica_groups=mesh['dp_0'=8,'dp_1'=4,'fsdp'=8] {'dp_0','dp_1'}, dimensions={0} | all-to-all | bytes 256 | tf_op jit(solution)/shard_map/all_to_all | solution.py:32
  280.0 8.6 %reduce-scatter.12.cloned.1.call-done = bf16[48,2048]{1,0:T(8,128)(2,1)} async-done(((bf16[192,2048]{1,0:T(8,128)(2,1)}), bf16[48,2048]{1,0:T(8,128)(2,1)}) %reduce-scatter.12.cloned.1.call-update) | async-done | bytes 196624
  288.7 1.9 copy.55
  290.6 2.1 fusion.36
  292.7 1.9 copy.50
  294.6 1.9 copy.51
  (124 shorter events, 40.7 us)
Async XLA Ops:
  7.2 52.2 %copy-start = (bf16[1536,1024]{1,0:T(8,128)(2,1)S(1)}, bf16[1536,1024]{1,0:T(8,128)(2,1)}, u32[]{:S(2)}) copy-start(bf16[1536,1024]{1,0:T(8,128)(2,1)} %param.32) | copy-start | bytes 9437188
  7.2 101.3 %reduce-scatter.8.cloned.1.call-start = ((), (), s32[]{:S(2)}) async-start(), calls=%async_computation.7 | async-start | bytes 5308416 | tf_op jit(solution)/shard_map/reduce_scatter | solution.py:230
  9.5 33.3 %collective-permute-start.4 = (s32[6]{0:T(128)S(1)}, s32[6]{0:T(128)S(1)}, u32[]{:S(2)}, u32[]{:S(2)}) collective-permute-start(s32[6]{0:T(128)S(1)} %broadcast_select_fusion.11), channel_id=1, source_target_pairs={{0,8},{8,16},{16,24},{24,32},{32,40},{40,48},{48,56},{56,64},{64,7... | collective-permute-start | bytes 80 | tf_op jit(solution)/shard_map/ppermute | solution.py:27
  18.9 27.6 %collective-permute-start = (bf16[6,2,4096]{2,1,0:T(2,128)(2,1)}, bf16[6,2,4096]{2,1,0:T(2,128)(2,1)}, u32[]{:S(2)}, u32[]{:S(2)}) collective-permute-start(bf16[6,2,4096]{2,1,0:T(2,128)(2,1)} %get-tuple-element.80), channel_id=1, source_target_pairs={{0,8},{8,16},{16,24},{24,32},{32,40},{40,48},{48,56},{56,64},{64,7... | collective-permute-start | bytes 294920 | tf_op jit(solution)/shard_map/ppermute | solution.py:27
  22.3 24.2 %collective-permute-start.2 = (bf16[6,2,4096]{2,1,0:T(2,128)(2,1)}, bf16[6,2,4096]{2,1,0:T(2,128)(2,1)}, u32[]{:S(2)}, u32[]{:S(2)}) collective-permute-start(bf16[6,2,4096]{2,1,0:T(2,128)(2,1)} %get-tuple-element.79), channel_id=1, source_target_pairs={{0,8},{8,16},{16,24},{24,32},{32,40},{40,48},{48,56},{56,64},{64,7... | collective-permute-start | bytes 294920 | tf_op jit(solution)/shard_map/ppermute | solution.py:27
  25.4 21.1 %collective-permute-start.3 = (bf16[6,2,4096]{2,1,0:T(2,128)(2,1)}, bf16[6,2,4096]{2,1,0:T(2,128)(2,1)}, u32[]{:S(2)}, u32[]{:S(2)}) collective-permute-start(bf16[6,2,4096]{2,1,0:T(2,128)(2,1)} %get-tuple-element.78), channel_id=1, source_target_pairs={{0,8},{8,16},{16,24},{24,32},{32,40},{40,48},{48,56},{56,64},{64,7... | collective-permute-start | bytes 294920 | tf_op jit(solution)/shard_map/ppermute | solution.py:27
  30.6 13.0 %collective-permute-start.1 = (s32[6,2]{1,0:T(8,128)S(1)}, s32[6,2]{1,0:T(8,128)S(1)}, u32[]{:S(2)}, u32[]{:S(2)}) collective-permute-start(s32[6,2]{1,0:T(8,128)S(1)} %broadcast_select_fusion.10), channel_id=1, source_target_pairs={{0,8},{8,16},{16,24},{24,32},{32,40},{40,48},{48,56},{56,64},{64,7... | collective-permute-start | bytes 152 | tf_op jit(solution)/shard_map/ppermute | solution.py:27
  43.8 2.6 copy-start.14
  51.6 2.1 copy-start.1
  52.2 2.9 copy-start.16
  55.2 2.6 copy-start.3
  57.8 1.6 copy-start.17
  65.0 0.7 copy-start.9
  65.0 12.9 %copy-start.15 = (s32[12]{0:T(128)S(1)}, s32[12]{0:T(128)}, u32[]{:S(2)}) copy-start(s32[12]{0:T(128)} %copy-done.14) | copy-start | bytes 148
  65.0 22.1 %copy-start.8 = (f32[12,1,1536]{2,1,0:T(1,128)S(1)}, f32[12,1,1536]{2,1,0:T(1,128)}, u32[]{:S(2)}) copy-start(f32[12,1,1536]{2,1,0:T(1,128)} %get-tuple-element.42) | copy-start | bytes 221188
  65.0 25.9 %copy-start.7 = (bf16[6,2,4096]{2,1,0:T(2,128)(2,1)S(1)}, bf16[6,2,4096]{2,1,0:T(2,128)(2,1)}, u32[]{:S(2)}) copy-start(bf16[6,2,4096]{2,1,0:T(2,128)(2,1)} %get-tuple-element.50) | copy-start | bytes 294916
  65.0 26.8 %copy-start.6 = (bf16[6,2,4096]{2,1,0:T(2,128)(2,1)S(1)}, bf16[6,2,4096]{2,1,0:T(2,128)(2,1)}, u32[]{:S(2)}) copy-start(bf16[6,2,4096]{2,1,0:T(2,128)(2,1)} %get-tuple-element.49) | copy-start | bytes 294916
  65.9 1.3 copy-start.10
  67.1 11.5 %copy-start.11 = (s32[6]{0:T(128)}, s32[6]{0:T(128)S(1)}, u32[]{:S(2)}) copy-start(s32[6]{0:T(128)S(1)} %iota_add_fusion) | copy-start | bytes 76
  67.8 20.9 %all-to-all-start.1 = ((s32[32,2,48]{2,1,0:T(2,128)}), s32[32,2,48]{2,1,0:T(2,128)}, u32[]{:S(2)}, u32[]{:S(2)}) async-start(s32[32,2,48]{2,1,0:T(2,128)} %broadcast_in_dim.118), calls=%async_computation.2 | async-start | bytes 65536 | tf_op jit(solution)/shard_map/all_to_all | solution.py:32
  88.7 22.4 %copy-start.5 = (bf16[1536,64]{0,1:T(8,128)(2,1)S(1)}, bf16[1536,64]{0,1:T(8,128)(2,1)}, u32[]{:S(2)}) copy-start(bf16[1536,64]{0,1:T(8,128)(2,1)} %param.33) | copy-start | bytes 589828
  91.8 25.1 %copy-start.12 = (s32[6]{0:T(128)S(1)}, s32[6]{0:T(128)}, u32[]{:S(2)}) copy-start(s32[6]{0:T(128)} %get-tuple-element.25) | copy-start | bytes 76
  91.8 25.1 %copy-start.13 = (s32[6]{0:T(128)S(1)}, s32[6]{0:T(128)}, u32[]{:S(2)}) copy-start(s32[6]{0:T(128)} %get-tuple-element.26) | copy-start | bytes 76
  110.2 0.8 copy-start.2
  113.3 8.5 %all-to-all-start = ((f32[8,1,12]{2,1,0:T(1,128)}), f32[8,1,12]{2,1,0:T(1,128)S(1)}, u32[]{:S(2)}, u32[]{:S(2)}) async-start(f32[8,1,12]{2,1,0:T(1,128)} %broadcast_in_dim.117), calls=%async_computation.1 | async-start | bytes 8192 | tf_op jit(solution)/shard_map/all_to_all | solution.py:32
  116.7 143.8 %reduce-scatter.10.cloned.1.call-start = ((), (), s32[]{:S(2)}) async-start(), calls=%async_computation.8 | async-start | bytes 7077888
  166.3 2.6 copy-start.18
  168.9 3.1 %copy-start.4 = (bf16[768,1536]{1,0:T(8,128)(2,1)S(1)}, bf16[768,1536]{1,0:T(8,128)(2,1)}, u32[]{:S(2)}) copy-start(bf16[768,1536]{1,0:T(8,128)(2,1)} %copy-done.3) | copy-start | bytes 7077892
  187.9 100.8 %reduce-scatter.12.cloned.1.call-start = ((), (), s32[]{:S(2)}) async-start(), calls=%async_computation.9 | async-start | bytes 983040
Sparse Core Ops, SparseCore 0:
  65.1 43.3 reduce-scatter.7
  188.0 72.4 reduce-scatter.9
  263.1 25.5 reduce-scatter.11
where the time goes:
time: 306 us; the launch traced here: 304 us
  waiting for transfers between devices  101 us (33%)
  blocking collectives  50 us (16%)
  local copies, waits for them, and re-layouts  48.1 us (16%)
  other arithmetic  35.7 us (12%)
  starting transfers between devices  30.7 us (10%)
  matrix products  22.1 us (7%)
  between operations  16.7 us (5%)
    unnamed x5, waiting for transfers between devices  81.3 us
    all_to_all x2, blocking collectives, sent_to_all(): lax.all_to_all(jnp.broadcast_to(x[None], (count, *x.shape)), axis, 0, 0,...  50 us
    unnamed x47, local copies, waits for them, and re-layouts  20.2 us
    ppermute x5, starting transfers between devices, shifted(): lax.ppermute(value, axis, [(source, source + steps) for source in range(i...  17 us
    gather x10, local copies, waits for them, and re-layouts, selection_mask(): return tuple((jnp.take(array, slot_list, axis=0) for array in local_data))  15.7 us
    reduce_scatter x1, waiting for transfers between devices, shards(): lax.psum_scatter(projected, 'fsdp', scatter_dimension=0, tiled=True)  14.9 us
    all_to_all x2, starting transfers between devices, sent_to_all(): lax.all_to_all(jnp.broadcast_to(x[None], (count, *x.shape)), axis, 0, 0,...  13.4 us
    mul x1, other arithmetic, backward(): coeff_rows * coeff_rows * error  7.93 us
  transfers between devices with their start and end apart: 10, of which 4 were waited for; matrix products, arithmetic and copies ran while one was open for 13% of the time, Pallas kernels for 0%

commit v1 on v0

v1 whole, which is shorter than its diff:
```python
import jax
import jax.numpy as jnp
from jax import lax
from jax.experimental import pallas as pl
from jax.experimental.pallas import tpu as pltpu
from jax.sharding import Mesh
from jax.sharding import PartitionSpec as P

MESH = pl.DeviceIdType.MESH
F32, BF16, I32 = jnp.float32, jnp.bfloat16, jnp.int32
NZ, NX, NY, NC = 8, 4, 4, 2
D, HID, TRAJ, SLOTS = 1536, 1024, 6, 12
UNITS, ROWS, CH = 12, 768, 192
KSTEPS = 10
SURV = 192
EPS = 1e-06
GELU_K = 0.7978845608028654
GELU_C = 0.044715


def tri(s):
    return lax.rem(s * s * s, 5)


def kernel(
    slot_s, src_s, cnt_s, src_v, slot_v, lat, noi, old, rank_v, time_v, wpatch, modl, wv, wup_h, wdn_h,
    out_up, out_dn, out_loss,
    meta, wup, wdn, snd_a, snd_b, rcv_a, rcv_b, meta_l, meta_all, meta_flat, tmp, xs, nz, od,
    mod_s, mod_c, mod_g, coef_u, adv_u, emb, modb, act, dg, dpre, dsend, drecv, pk, ysend, yrecv, pfull,
    fin, finb, inv, ups, mod_t, up_t, gu, gd, zr, xr, s2u, s2d, s2ur, s2dr, loss_own, loss_x, loss_z,
    lsem, ssem, rsem,
):
    z, x, y, c = (lax.axis_index(n) for n in ("z", "x", "y", "c"))
    owner = z * NX + x

    def dev(dz=0, dx=0, dy=0, dc=0):
        return (
            lax.rem(z + (dz + NZ), NZ),
            lax.rem(x + (dx + NX), NX),
            lax.rem(y + (dy + NY), NY),
            lax.rem(c + dc, NC),
        )

    nxt = lax.rem(owner + 1, NZ * NX)
    prv = lax.rem(owner + NZ * NX - 1, NZ * NX)
    next_dev = (nxt // NX, lax.rem(nxt, NX), y, c)
    prev_dev = (prv // NX, lax.rem(prv, NX), y, c)

    ids = {}

    def mid(name):
        return ids.setdefault(name, len(ids))

    sent = []

    def copy(name, src, dst, to):
        i = mid(name) if isinstance(name, str) else name
        return pltpu.make_async_remote_copy(
            src_ref=src, dst_ref=dst, send_sem=ssem.at[i], recv_sem=rsem.at[i],
            device_id=to, device_id_type=MESH,
        )

    def send(name, src, dst, to):
        d = copy(name, src, dst, to)
        d.start()
        sent.append(d)

    def recv(name, dst, to=None):
        copy(name, dst, dst, dev(dc=1) if to is None else to).wait_recv()

    barrier = pltpu.get_barrier_semaphore()
    peers = [dev(dx=i) for i in range(1, NX)] + [dev(dz=i) for i in range(1, NZ)]
    peers += [dev(dy=1), dev(dy=-1), dev(dc=1), next_dev, prev_dev]
    meta[0:1, 0:SLOTS] = rank_v[...]
    meta[1:3, 0:SLOTS] = time_v[...]
    for p in peers:
        pl.semaphore_signal(barrier, inc=1, device_id=p, device_id_type=MESH)
    cp_up = pltpu.make_async_copy(wup_h, wup, lsem.at[0])
    cp_dn = pltpu.make_async_copy(wdn_h, wdn, lsem.at[1])
    cp_up.start()
    cp_dn.start()
    lead_n = jnp.minimum(owner + 1, NZ * NX - 1) * TRAJ
    lead = owner * TRAJ
    for i in range(TRAJ):
        s = slot_s[lead_n + i]
        snd_a[i] = lat[s]
        snd_b[0, i] = noi[s]
        snd_b[1, i] = old[s]
    meta_all[z * NX + x] = meta[...]
    pl.semaphore_wait(barrier, len(peers))

    send("meta_l", meta, meta_l, next_dev)
    send("shift_a", snd_a, rcv_a, next_dev)
    send("shift_b", snd_b, rcv_b, next_dev)
    for i in range(1, NX):
        send(f"meta_x{i}", meta, meta_all.at[z * NX + x], dev(dx=i))

    slots = [slot_s[lead + i] for i in range(TRAJ)]
    lefts = [src_s[lead + i] != owner for i in range(TRAJ)]

    sub = lax.broadcasted_iota(I32, (16, 128), 0)
    lane = lax.broadcasted_iota(I32, (16, 128), 1)
    pos = jnp.zeros((16, 128), I32)
    from_left = jnp.zeros((16, 128), I32)
    for i in range(TRAJ):
        mine = (sub >> 1) == i
        pos = pos + jnp.where(mine, slots[i], 0)
        from_left = from_left + jnp.where(mine, lefts[i].astype(I32), 0)
    recv("meta_l", meta_l)

    def step_row(n):
        wide = [jnp.broadcast_to(m[n : n + 1, :], (16, 128)) for m in (meta_l, meta)]
        return jnp.where(from_left == 1, wide[0], wide[1])

    row = jnp.where((sub & 1) == 0, step_row(1), step_row(2))
    stamp = jnp.sum(jnp.where(lane == pos, row.astype(F32), 0.0), axis=1, keepdims=True)
    level = 1.0 - stamp * (1.0 / KSTEPS)
    coef = jnp.sqrt((1.0 / KSTEPS) * (1.0 - level + (1.0 / KSTEPS)) / level) / 0.7
    coef_u[...] = jnp.broadcast_to(coef, (16, 128))
    for kind, dst in ((0, mod_s), (1, mod_c), (2, mod_g)):
        acc = jnp.zeros((16, D), F32)
        for t in range(KSTEPS):
            acc = jnp.where(stamp == float(t), jnp.broadcast_to(modl[t, pl.ds(kind, 1), :], (16, D)), acc)
        dst[...] = acc + 1.0 if kind == 1 else acc

    def assemble(own, arrived, i):
        v = jnp.where(lefts[i], arrived.astype(F32), own.astype(F32))
        tmp[...] = v
        return tmp[pl.ds(0, 32, stride=2), :], tmp[pl.ds(1, 32, stride=2), :]

    recv("shift_a", rcv_a)
    for i in range(TRAJ):
        for step, v in enumerate(assemble(lat[slots[i]], rcv_a[i], i)):
            u = 2 * i + step
            xs[u // 3, (u % 3) * 32 : (u % 3) * 32 + 32, :] = v

    def spread(pair):
        return jnp.concatenate([pair[:, :64], pltpu.roll(pair, 64, 1)[:, :64]], axis=0)

    cp_up.wait()
    cp_dn.wait()

    def forward(s, carry):
        k = lax.rem(y + 2 + tri(s), NY)
        r0 = pl.multiple_of(k * CH, CH)
        emb[pl.ds(r0, CH), :] = jnp.dot(spread(xs[k]).astype(BF16), wpatch[...], preferred_element_type=F32)

        def norm(b, carry):
            rb = pl.multiple_of(r0 + b * 32, 32)
            u = k * 3 + lax.rem(b, 3)
            v = emb[pl.ds(rb, 32), :]
            v = v - jnp.mean(v, axis=-1, keepdims=True)
            i = lax.rsqrt(jnp.mean(v * v, axis=-1, keepdims=True) + EPS)
            modb[pl.ds(rb, 32), :] = (v * i * mod_c[pl.ds(u, 1), :] + mod_s[pl.ds(u, 1), :]).astype(BF16)
            return carry

        lax.fori_loop(0, 6, norm, 0)

        def up(n, carry):
            cols = pl.ds(pl.multiple_of(n * 512, 512), 512)
            pre = jnp.dot(modb[pl.ds(r0, CH), :], wup[:, cols], preferred_element_type=F32)
            sq = pre * pre
            th = jnp.tanh(GELU_K * (pre + GELU_C * (sq * pre)))
            half = 0.5 * (1.0 + th)
            act[pl.ds(r0, CH), cols] = (pre * half).astype(BF16)
            dg[pl.ds(r0, CH), cols] = half + (0.5 * GELU_K) * pre * (1.0 - th * th) * (1.0 + 3.0 * GELU_C * sq)
            return carry

        lax.fori_loop(0, 2, up, 0)

        def down(n, carry):
            q = pl.multiple_of(n * 768, 768)
            v = lax.dot_general(
                act[pl.ds(r0, CH), :], wdn[pl.ds(q, 768), :], (((1,), (1,)), ((), ())), preferred_element_type=F32
            )

            @pl.when(n == c)
            def _():
                pk[s, 0] = v[:, :384]
                pk[s, 1] = v[:, 384:]

            @pl.when(n != c)
            def _():
                dsend[s, 0] = v[:, :384].astype(BF16)
                dsend[s, 1] = v[:, 384:].astype(BF16)

            return carry

        lax.fori_loop(0, 2, down, 0)
        copy(d2d + s, dsend.at[s], drecv.at[s], dev(dc=1)).start()

        @pl.when(s == 1)
        def _():
            presum(0)
            ysend[0] = pk[0, 0].astype(BF16)
            ysend[1] = pk[0, 1].astype(BF16)
            copy("y1a", ysend.at[0], yrecv.at[0], dev(dy=1)).start()
            copy("y1b", ysend.at[1], yrecv.at[1], dev(dy=-1)).start()

        @pl.when(s == 2)
        def _():
            presum(1)
            ysend[2] = pk[1, 0].astype(BF16)
            copy("y2a", ysend.at[2], yrecv.at[2], dev(dy=-1)).start()

        @pl.when(s == 3)
        def _():
            presum(2)
            ysend[3] = pk[2, 1].astype(BF16)
            copy("y2b", ysend.at[3], yrecv.at[3], dev(dy=1)).start()
            recv("y1b", yrecv.at[1])
            ysend[4] = (pk[1, 1] + yrecv[1].astype(F32)).astype(BF16)
            copy("y3b", ysend.at[4], yrecv.at[4], dev(dy=-1)).start()
            recv("y1a", yrecv.at[0])
            ysend[5] = (pk[2, 0] + yrecv[0].astype(F32)).astype(BF16)
            copy("y3a", ysend.at[5], yrecv.at[5], dev(dy=1)).start()

        return carry

    d2d = mid("d2d0")
    for i in range(1, 4):
        mid(f"d2d{i}")

    def presum(s):
        recv(d2d + s, drecv.at[s])
        for h in range(2):
            pk[s, h] = pk[s, h] + drecv[s, h].astype(F32)

    lax.fori_loop(0, 4, forward, 0)
    for i in range(4):
        sent.append(copy(d2d + i, dsend.at[i], drecv.at[i], dev(dc=1)))
    for i, (n, t) in enumerate((("y1a", 1), ("y1b", -1), ("y2a", -1), ("y2b", 1), ("y3b", -1), ("y3a", 1))):
        sent.append(copy(n, ysend.at[i], yrecv.at[i], dev(dy=t)))

    for i in range(1, NX):
        recv(f"meta_x{i}", meta_all.at[z * NX + lax.rem(x + NX - i, NX)])
    for i in range(1, NZ):
        send(f"meta_z{i}", meta_all.at[pl.ds(z * NX, NX)], meta_all.at[pl.ds(z * NX, NX)], dev(dz=i))

    def transpose_pair(p, src, put):
        tok = pl.ds(pl.multiple_of(p * 384, 384), 384)
        for b in range(4):
            put(b, tok, src[tok, 384 * b : 384 * b + 384].T)

    def put_mod(b, tok, t):
        mod_t[2 * b, :, tok] = t[:192]
        mod_t[2 * b + 1, :, tok] = t[192:]

    def put_up(b, tok, t):
        for zz in range(2):
            for xx in range(NX):
                o = zz * 192 + xx * 48
                up_t[xx, (2 * b + zz) * 48 : (2 * b + zz) * 48 + 48, tok] = t[o : o + 48]

    def both(p, carry):
        transpose_pair(p, modb, put_mod)
        return carry

    presum(3)
    lax.fori_loop(0, 2, both, 0)

    q0 = 2 * c
    recv("y2a", yrecv.at[2])
    recv("y3a", yrecv.at[5])
    pfull[y, q0] = (pk[3, 0] + yrecv[2].astype(F32) + yrecv[5].astype(F32)).astype(BF16)
    send("g_up_a", pfull.at[y, q0], pfull.at[y, q0], dev(dy=1))
    recv("y2b", yrecv.at[3])
    recv("y3b", yrecv.at[4])
    pfull[y, q0 + 1] = (pk[3, 1] + yrecv[3].astype(F32) + yrecv[4].astype(F32)).astype(BF16)
    send("g_dn_b", pfull.at[y, q0 + 1], pfull.at[y, q0 + 1], dev(dy=-1))
    send("g_up_b", pfull.at[y, q0 + 1], pfull.at[y, q0 + 1], dev(dy=1))
    send("g_dn_a", pfull.at[y, q0], pfull.at[y, q0], dev(dy=-1))
    send("c_own", pfull.at[y, pl.ds(q0, 2)], pfull.at[y, pl.ds(q0, 2)], dev(dc=1))

    recv("shift_b", rcv_b)
    for i in range(TRAJ):
        for arr, which, dst in ((noi, 0, nz), (old, 1, od)):
            for step, v in enumerate(assemble(arr[slots[i]], rcv_b[which, i], i)):
                u = 2 * i + step
                dst[u // 3, (u % 3) * 32 : (u % 3) * 32 + 32, :] = v

    for i in range(1, NZ):
        recv(f"meta_z{i}", meta_all.at[pl.ds(lax.rem(z + NZ - i, NZ) * NX, NX)])
    for r in range(NZ * NX):
        meta_flat[r : r + 1, :] = meta_all[r, 0:1, :]
    ranks = meta_flat[...]
    hot = (lax.broadcasted_iota(I32, (NZ * NX, SURV), 0) == src_v[...]).astype(F32).astype(BF16)
    first = (((0,), (0,)), ((), ()))
    hi = lax.dot_general((ranks >> 4).astype(F32).astype(BF16), hot, first, preferred_element_type=F32)[:16]
    lo = lax.dot_general((ranks & 15).astype(F32).astype(BF16), hot, first, preferred_element_type=F32)[:16]
    by_slot = hi * 16.0 + lo
    rank = jnp.sum(
        jnp.where(lax.broadcasted_iota(I32, (16, SURV), 0) == slot_v[...], by_slot, 0.0), axis=0, keepdims=True
    )
    rank_i = rank.astype(I32)
    sq_i = rank_i * rank_i
    sq_hi, sq_lo = (sq_i >> 10).astype(F32), (sq_i & 1023).astype(F32)
    jdx = lax.broadcasted_iota(I32, (1, SURV), 1)

    def bounds(g, carry):
        end = carry[0] + cnt_s[g]
        out = [end]
        for i in range(TRAJ):
            hit = (lead + i >= carry[0]) & (lead + i < end)
            out += [jnp.where(hit, carry[0], carry[1 + 2 * i]), jnp.where(hit, end, carry[2 + 2 * i])]
        return tuple(out)

    ends = lax.fori_loop(0, 48, bounds, (jnp.int32(0),) * (1 + 2 * TRAJ))
    for i in range(TRAJ):
        lo_i, hi_i = ends[1 + 2 * i], ends[2 + 2 * i]
        inside = (jdx >= lo_i) & (jdx < hi_i)

        def total(v):
            return jnp.sum(jnp.where(inside, v, 0.0), axis=1, keepdims=True)

        s1 = total(rank)
        s1_i = s1.astype(I32)
        s2_i = total(sq_hi).astype(I32) * 1024 + total(sq_lo).astype(I32)
        n_i = jnp.full((1, 1), hi_i - lo_i, I32)
        n = n_i.astype(F32)
        r = jnp.sum(jnp.where(jdx == lead + i, rank, 0.0), axis=1, keepdims=True)
        dev_i = jnp.sqrt((n_i * s2_i - s1_i * s1_i).astype(F32)) / n
        a = (r - s1 / n) / jnp.maximum(dev_i, 1.0)
        adv_u[2 * i : 2 * i + 2, :] = jnp.broadcast_to(a, (2, 128))

    loss_own[...] = jnp.zeros((1, 128), F32)

    def head(k):
        r0 = pl.multiple_of(k * CH, CH)

        def mix(b, carry):
            o = pl.multiple_of(b * 32, 32)
            u = k * 3 + lax.rem(b, 3)
            proj = jnp.concatenate([pfull[k, q, pl.ds(o, 32), :] for q in range(4)], axis=1).astype(F32)
            v = emb[pl.ds(pl.multiple_of(r0 + o, 32), 32), :] + mod_g[pl.ds(u, 1), :] * proj
            v = v - jnp.mean(v, axis=-1, keepdims=True)
            i = lax.rsqrt(jnp.mean(v * v, axis=-1, keepdims=True) + EPS)
            v = v * i
            fin[pl.ds(o, 32), :] = v
            finb[pl.ds(o, 32), :] = v.astype(BF16)
            inv[pl.ds(o, 32), :] = jnp.broadcast_to(i, (32, 128))
            return carry

        lax.fori_loop(0, 6, mix, 0)
        velocity = lax.dot_general(finb[...], wv[...], (((1,), (1,)), ((), ())), preferred_element_type=F32)
        drawn, target = spread(nz[k]), spread(od[k])
        err = velocity - target
        dv = [None] * 6
        for j in range(3):
            u = k * 3 + j
            cu = coef_u[pl.ds(u, 1), :][:, :64]
            au = adv_u[pl.ds(u, 1), :][:, :1]
            part = jnp.zeros((32, 64), F32)
            for h in range(2):
                o = h * 96 + j * 32
                e, n = err[o : o + 32], drawn[o : o + 32]
                part = part + cu * n * e + 0.5 * cu * cu * e * e
            logratio = -jnp.sum(jnp.sum(part, axis=0, keepdims=True), axis=1, keepdims=True) * (1.0 / 4096)
            ratio = jnp.exp(logratio)
            plain = ratio * au
            bounded = jnp.clip(ratio, 0.8, 1.2) * au
            loss_own[...] += jnp.broadcast_to(-jnp.minimum(plain, bounded), (1, 128))
            slope = jnp.where(plain <= bounded, -au * ratio * (1.0 / (SURV * 2)), 0.0)
            for h in range(2):
                o = h * 96 + j * 32
                e, n = err[o : o + 32], drawn[o : o + 32]
                dv[h * 3 + j] = slope * (-(cu * n + cu * cu * e) * (1.0 / 4096))
        dvel = jnp.concatenate(dv, axis=0).astype(BF16)
        dfin = jnp.dot(dvel, wv[...], preferred_element_type=F32)
        pk[0, 0], pk[0, 1] = dfin[:, :384], dfin[:, 384:768]
        pk[1, 0], pk[1, 1] = dfin[:, 768:1152], dfin[:, 1152:]

        def back(b, carry):
            o = pl.multiple_of(b * 32, 32)
            u = k * 3 + lax.rem(b, 3)
            g = jnp.concatenate([pk[q // 2, q % 2, pl.ds(o, 32), :] for q in range(4)], axis=1)
            f = fin[pl.ds(o, 32), :]
            m1 = jnp.mean(g, axis=-1, keepdims=True)
            m2 = jnp.mean(g * f, axis=-1, keepdims=True)
            i = inv[pl.ds(o, 32), :][:, :1]
            ups[pl.ds(pl.multiple_of(r0 + o, 32), 32), :] = (
                mod_g[pl.ds(u, 1), :] * (i * (g - m1 - f * m2))
            ).astype(BF16)
            return carry

        lax.fori_loop(0, 6, back, 0)

    def dact(k):
        rows = pl.ds(pl.multiple_of(k * CH, CH), CH)

        def one(n, carry):
            cols = pl.ds(pl.multiple_of(n * 512, 512), 512)
            v = jnp.dot(ups[rows, :], wdn[:, cols], preferred_element_type=F32)
            dpre[rows, cols] = (v * dg[rows, cols]).astype(BF16)
            return carry

        lax.fori_loop(0, 2, one, 0)

    yu, yd, yo = (lax.rem(y + i, NY) for i in (1, 3, 2))
    p0 = 2 - 2 * c

    def fwd_core(name, k, q):
        copy(name, pfull.at[k, q], pfull.at[k, q], dev(dc=1)).start()

    def got(name, k, q):
        recv(name, pfull.at[k, q])

    def visit(h, carry):
        k = lax.rem(y + tri(h), NY)

        @pl.when(h == 0)
        def _():
            recv("c_own", pfull.at[y, pl.ds(p0, 2)])

        @pl.when(h == 1)
        def _():
            got("g_dn_a", yu, q0)
            fwd_core("c_ua", yu, q0)
            got("c_ua", yu, p0)
            got("c_ub", yu, p0 + 1)

        @pl.when(h == 2)
        def _():
            got("g_up_b", yd, q0 + 1)
            fwd_core("c_db", yd, q0 + 1)
            got("c_da", yd, p0)
            got("c_db", yd, p0 + 1)

        @pl.when(h == 3)
        def _():
            got("r_up", yo, q0)
            fwd_core("c_oa", yo, q0)
            got("r_dn", yo, q0 + 1)
            fwd_core("c_ob", yo, q0 + 1)
            got("c_oa", yo, p0)
            got("c_ob", yo, p0 + 1)

        head(k)

        @pl.when(h == 0)
        def _():
            got("g_up_a", yd, q0)
            copy("r_up", pfull.at[yd, q0], pfull.at[yd, q0], dev(dy=1)).start()
            fwd_core("c_da", yd, q0)
            got("g_dn_b", yu, q0 + 1)
            copy("r_dn", pfull.at[yu, q0 + 1], pfull.at[yu, q0 + 1], dev(dy=-1)).start()
            fwd_core("c_ub", yu, q0 + 1)

        dact(k)
        return carry

    lax.fori_loop(0, 4, visit, 0)
    sent.append(copy("r_up", pfull.at[yd, q0], pfull.at[yd, q0], dev(dy=1)))
    sent.append(copy("r_dn", pfull.at[yu, q0 + 1], pfull.at[yu, q0 + 1], dev(dy=-1)))
    for n, k, q in (("c_ua", yu, q0), ("c_ub", yu, q0 + 1), ("c_da", yd, q0), ("c_db", yd, q0 + 1),
                    ("c_oa", yo, q0), ("c_ob", yo, q0 + 1)):
        sent.append(copy(n, pfull.at[k, q], pfull.at[k, q], dev(dc=1)))

    def both_up(p, carry):
        transpose_pair(p, ups, put_up)
        return carry

    lax.fori_loop(0, 2, both_up, 0)

    def grad_dn(k):
        for h in range(2):
            gd[k, h] = jnp.dot(up_t[k], act[:, 512 * h : 512 * h + 512], preferred_element_type=F32).astype(BF16)

    def grad_up(k):
        for h in range(2):
            gu[k, h] = jnp.dot(mod_t[k], dpre[:, 512 * h : 512 * h + 512], preferred_element_type=F32).astype(BF16)

    def at(axis_pos, n, off):
        return lax.rem(axis_pos + (off + n), n)

    xsend = lambda name, off, h, to: copy(name, gd.at[at(x, NX, off), h], xr.at[xi[name]], dev(dx=to))
    xi = {"xa1": 0, "xb1": 1, "xa2": 2, "wb1": 3, "wa1": 4, "wb2": 5}
    xspec = {"xa1": (2, 0, 1), "xb1": (1, 1, 1), "xa2": (1, 0, 1), "wb1": (2, 1, -1), "wa1": (-1, 0, -1), "wb2": (-1, 1, -1)}

    def xgo(name):
        off, h, to = xspec[name]
        xsend(name, off, h, to).start()

    def dn_step(s, carry):
        grad_dn(lax.rem(x + 2 + tri(s), NX))

        @pl.when(s == 0)
        def _():
            xgo("xa1")
            xgo("wb1")

        @pl.when(s == 1)
        def _():
            xgo("wa1")

        @pl.when(s == 2)
        def _():
            xgo("xb1")

        return carry

    zi = {}
    zspec = {}
    for d, sign in (("r", 1), ("l", -1)):
        for h in range(2):
            far = (h == 0) == (sign == 1)
            for s in range(1, 5 if far else 4):
                off = sign * ((5 - s) if far else (4 - s))
                zi[f"z{d}{h}{s}"] = len(zi)
                zspec[f"z{d}{h}{s}"] = (off, h, sign)

    def zcopy(name):
        off, h, to = zspec[name]
        return copy(name, gu.at[at(z, NZ, off), h], zr.at[zi[name]], dev(dz=to))

    def up_step(t, off):
        grad_up(lax.rem(z + off, NZ))

        @pl.when(t == 0)
        def _():
            zcopy("zr01").start()
            zcopy("zl11").start()

        @pl.when(t == 1)
        def _():
            zcopy("zr11").start()

        @pl.when(t == 2)
        def _():
            zcopy("zl01").start()

        return off + (t + 1) * (2 * lax.rem(t, 2) - 1)

    lax.fori_loop(0, 4, dn_step, 0)
    lax.fori_loop(0, 8, up_step, 4)

    for i in range(1, NX):
        send(f"loss_x{i}", loss_own, loss_x.at[i], dev(dx=i))

    def zrelay(prev, name):
        off, h, _ = zspec[name]
        k = at(z, NZ, off)
        recv(prev, zr.at[zi[prev]])
        gu[k, h] = (gu[k, h].astype(F32) + zr[zi[prev]].astype(F32)).astype(BF16)
        zcopy(name).start()

    def xrelay(prev, name):
        off, h, to = xspec[name]
        k = at(x, NX, off)
        recv(prev, xr.at[xi[prev]])
        gd[k, h] = (gd[k, h].astype(F32) + xr[xi[prev]].astype(F32)).astype(BF16)
        xgo(name)

    zrelay("zr01", "zr02")
    zrelay("zl11", "zl12")
    zrelay("zr11", "zr12")
    zrelay("zl01", "zl02")
    xrelay("xa1", "xa2")
    xrelay("wb1", "wb2")
    lsum = loss_own[...]
    for i in range(1, NX):
        recv(f"loss_x{i}", loss_x.at[i])
        lsum = lsum + loss_x[i]
    loss_z[0] = lsum
    for i in range(1, NZ):
        send(f"loss_z{i}", loss_z.at[0], loss_z.at[i], dev(dz=i))
    zrelay("zr02", "zr03")
    zrelay("zl12", "zl13")
    zrelay("zr12", "zr13")
    zrelay("zl02", "zl03")
    zrelay("zr03", "zr04")
    zrelay("zl13", "zl14")

    def finish_x(h, names):
        v = gd[x, h].astype(F32)
        for n in names:
            recv(n, xr.at[xi[n]])
            v = v + xr[xi[n]].astype(F32)
        v = v.astype(BF16)
        for i in range(NZ):
            s2d[i, h] = v[48 * i : 48 * i + 48]

    def finish_z(h, names):
        v = gu[z, h].astype(F32)
        for n in names:
            recv(n, zr.at[zi[n]])
            v = v + zr[zi[n]].astype(F32)
        v = v.astype(BF16)
        for i in range(NX):
            s2u[i, h] = v[48 * i : 48 * i + 48]

    def dcopy(name):
        off, h, to = zspec[name]
        return copy("s" + name, s2d.at[at(z, NZ, off), h], s2dr.at[zi[name]], dev(dz=to))

    def drelay(prev, name):
        off, h, _ = zspec[name]
        k = at(z, NZ, off)
        recv("s" + prev, s2dr.at[zi[prev]])
        s2d[k, h] = (s2d[k, h].astype(F32) + s2dr[zi[prev]].astype(F32)).astype(BF16)
        dcopy(name).start()

    def ucopy(name):
        off, h, to = xspec[name]
        return copy("s" + name, s2u.at[at(x, NX, off), h], s2ur.at[xi[name]], dev(dx=to))

    def urelay(prev, name):
        off, h, _ = xspec[name]
        k = at(x, NX, off)
        recv("s" + prev, s2ur.at[xi[prev]])
        s2u[k, h] = (s2u[k, h].astype(F32) + s2ur[xi[prev]].astype(F32)).astype(BF16)
        ucopy(name).start()

    finish_x(0, ("xa2", "wa1"))
    dcopy("zr01").start()
    dcopy("zl01").start()
    finish_x(1, ("xb1", "wb2"))
    dcopy("zl11").start()
    dcopy("zr11").start()
    finish_z(1, ("zr13", "zl14"))
    ucopy("wb1").start()
    ucopy("xb1").start()
    finish_z(0, ("zr04", "zl03"))
    ucopy("xa1").start()
    ucopy("wa1").start()
    drelay("zr01", "zr02")
    drelay("zl01", "zl02")
    drelay("zl11", "zl12")
    drelay("zr11", "zr12")
    urelay("wb1", "wb2")
    urelay("xa1", "xa2")
    drelay("zr02", "zr03")
    drelay("zl02", "zl03")
    drelay("zl12", "zl13")
    drelay("zr12", "zr13")
    drelay("zr03", "zr04")
    drelay("zl13", "zl14")
    lsum = loss_z[0]
    for i in range(1, NZ):
        recv(f"loss_z{i}", loss_z.at[i])
        lsum = lsum + loss_z[i]
    out_loss[...] = lsum * (1.0 / (SURV * 2))
    for h, names in ((0, ("xa2", "wa1")), (1, ("xb1", "wb2"))):
        v = s2u[x, h].astype(F32)
        for n in names:
            recv("s" + n, s2ur.at[xi[n]])
            v = v + s2ur[xi[n]].astype(F32)
        out_up[:, 512 * h : 512 * h + 512] = v
    for h, names in ((0, ("zr04", "zl03")), (1, ("zr13", "zl14"))):
        v = s2d[z, h].astype(F32)
        for n in names:
            recv("s" + n, s2dr.at[zi[n]])
            v = v + s2dr[zi[n]].astype(F32)
        out_dn[:, 512 * h : 512 * h + 512] = v

    for n in xspec:
        sent.append(xsend(n, *xspec[n]))
        sent.append(ucopy(n))
    for n in zspec:
        sent.append(zcopy(n))
        sent.append(dcopy(n))
    for d in sent:
        d.wait_send()
    assert len(ids) <= NSEM, len(ids)


NSEM = 104


def shards(
    latents, noise, behavior_velocity, timestep, reward_rank_integer, surviving_source_index,
    surviving_slot_index, group_kept_count, patch_input_weight, modulation_lookup,
    up_projection_weight, down_projection_weight, velocity_head_weight,
):
    def pairs(a):
        return a.reshape(SLOTS, 2, 32, 128).transpose(0, 2, 1, 3).reshape(SLOTS, 64, 128)

    smem = pl.BlockSpec(memory_space=pltpu.SMEM)
    vmem = pl.BlockSpec(memory_space=pltpu.VMEM)
    hbm = pl.BlockSpec(memory_space=pl.ANY)
    V = pltpu.VMEM
    piece = (CH, 384)
    scratch = [
        V((8, 128), I32), V((D, HID), BF16), V((D, HID), BF16),
        V((TRAJ, 64, 128), BF16), V((2, TRAJ, 64, 128), BF16), V((TRAJ, 64, 128), BF16), V((2, TRAJ, 64, 128), BF16),
        V((8, 128), I32), V((NZ * NX, 8, 128), I32), V((NZ * NX, 128), I32), V((64, 128), F32),
        V((4, 96, 128), F32), V((4, 96, 128), F32), V((4, 96, 128), F32),
        V((16, D), F32), V((16, D), F32), V((16, D), F32), V((16, 128), F32), V((16, 128), F32),
        V((ROWS, D), F32), V((ROWS, D), BF16), V((ROWS, HID), BF16), V((ROWS, HID), F32), V((ROWS, HID), BF16),
        V((4, 2, *piece), BF16), V((4, 2, *piece), BF16), V((4, 2, *piece), F32),
        V((6, *piece), BF16), V((6, *piece), BF16), V((4, 4, *piece), BF16),
        V((CH, D), F32), V((CH, D), BF16), V((CH, 128), F32), V((ROWS, D), BF16),
        V((NZ, 192, ROWS), BF16), V((NX, 384, ROWS), BF16),
        V((NZ, 2, 192, 512), BF16), V((NX, 2, 384, 512), BF16), V((14, 192, 512), BF16), V((6, 384, 512), BF16),
        V((NX, 2, 48, 512), BF16), V((NZ, 2, 48, 512), BF16), V((6, 48, 512), BF16), V((14, 48, 512), BF16),
        V((1, 128), F32), V((NX, 1, 128), F32), V((NZ, 1, 128), F32),
        pltpu.SemaphoreType.DMA((2,)), pltpu.SemaphoreType.DMA((NSEM,)), pltpu.SemaphoreType.DMA((NSEM,)),
    ]
    up, dn, loss = pl.pallas_call(
        kernel,
        out_shape=(
            jax.ShapeDtypeStruct((48, HID), F32),
            jax.ShapeDtypeStruct((48, HID), F32),
            jax.ShapeDtypeStruct((1, 128), F32),
        ),
        in_specs=[smem] * 3 + [vmem] * 10 + [hbm] * 2,
        out_specs=(vmem,) * 3,
        scratch_shapes=scratch,
        compiler_params=pltpu.CompilerParams(collective_id=0, has_side_effects=True, vmem_limit_bytes=67043328),
    )(
        surviving_slot_index, surviving_source_index, group_kept_count,
        surviving_source_index.reshape(1, SURV), surviving_slot_index.reshape(1, SURV),
        pairs(latents), pairs(noise), pairs(behavior_velocity), reward_rank_integer.reshape(1, SLOTS), timestep.T,
        patch_input_weight, modulation_lookup, velocity_head_weight.T,
        up_projection_weight, down_projection_weight,
    )
    return up, dn, loss[0, 0]


def solution(mesh):
    finer = Mesh(mesh.devices.reshape(NZ, NX, NY, NC), ("z", "x", "y", "c"))
    dp, fs = ("z", "x"), ("y", "c")
    in_specs = (
        P(dp, None, None), P(dp, None, None), P(dp, None, None), P(dp, None), P(dp), P(), P(), P(), P(), P(),
        P(None, fs), P(None, fs), P(),
    )
    out_specs = (P(dp, fs), P(dp, fs), P())
    return jax.shard_map(shards, mesh=finer, in_specs=in_specs, out_specs=out_specs, check_vma=False)
```

time: 306 us -> 122 us (0.40)
  Pallas kernels: 0 us -> 116 us
  waiting for transfers between devices: 101 us -> 0 us
  blocking collectives: 50 us -> 0 us
  local copies, waits for them, and re-layouts: 48.1 us -> 3.23 us
  other arithmetic: 35.7 us -> 0 us
  starting transfers between devices: 30.7 us -> 0 us
  matrix products: 22.1 us -> 0 us
  between operations: 16.7 us -> 2.4 us
    pallas_call x0 -> x1, Pallas kernels: none -> 116 us  [shards(): pl.pallas_call(kernel, out_shape=(jax.ShapeDtypeStruct((48, HID), F32), j...]
    unnamed x5 -> x0, waiting for transfers between devices: 81.3 us -> none
    all_to_all x2 -> x0, blocking collectives: 50 us -> none  [sent_to_all(): lax.all_to_all(jnp.broadcast_to(x[None], (count, *x.shape)), axis, 0, 0,...]
    dot_general x8 -> x0, matrix products: 22.1 us -> none  [the longest x1 5.57 us: shards(): lax.dot_general(activated, down_projection_weight, (((1,), (1,)), ((), ()...]
    gather x14 -> x0, local copies, waits for them, and re-layouts: 20.3 us -> none  [the longest x10 15.7 us: selection_mask(): return tuple((jnp.take(array, slot_list, axis=0) for array in local_data))]
    ppermute x5 -> x0, starting transfers between devices: 17 us -> none  [shifted(): lax.ppermute(value, axis, [(source, source + steps) for source in range(i...]
    unnamed x47 -> x2, local copies, waits for them, and re-layouts: 20.2 us -> 3.23 us
    mul x4 -> x0, other arithmetic: 16.7 us -> none  [the longest x1 7.93 us: backward(): coeff_rows * coeff_rows * error]
  transfers between devices with their start and end apart: 10 -> 0, of which waited for: 4 -> 0; matrix products, arithmetic and copies ran while one was open for 13% -> 0% of each run, Pallas kernels for 0% -> 0%
where the time goes in v1:
time: 122 us
  Pallas kernels  116 us (95%)
  local copies, waits for them, and re-layouts  3.23 us (3%)
  between operations  2.4 us (2%)
    pallas_call x1, Pallas kernels, shards(): pl.pallas_call(kernel, out_shape=(jax.ShapeDtypeStruct((48, HID), F32), j...  116 us
    unnamed x2, local copies, waits for them, and re-layouts  3.23 us

profile of v1, /device:TPU:32, one launch (start us, length us, event | category | flops | bytes accessed | tf_op | source)
XLA Modules:
  0.0 121.7 jit_solution(14149581521263509965)
XLA Ops:
  0.6 116.1 %shard_map.148 = (f32[48,1024]{1,0:T(8,128)}, f32[48,1024]{1,0:T(8,128)}, f32[1,128]{1,0:T(1,128)}) custom-call(s32[192]{0:T(256)} %slot_s.1, s32[192]{0:T(256)} %src_s.1, s32[48]{0:T(128)} %cnt_s.1, s32[1,192]{1,0:T(1,128)} %bitcast.27, s32[1,192]{1,0:T(1,128)} %bitcast.26, bf16[12,64,128]{2,1,0:T(8,128)(2,1)} %bitcast.22, bf16[12,64,128]{2,1,0:T(8,128)(2,1)} %bitcast.23, ...), custom_call_target="tpu_custom_call" | custom-call | tf_op jit(solution)/shard_map/pallas_call | solution.py:699
  116.8 1.6 %copy.22 = f32[48,1024]{1,0:T(8,128)} copy(f32[48,1024]{1,0:T(8,128)} %get-tuple-element.12) | data formatting | bytes 393216
  118.4 1.6 %copy.23 = f32[48,1024]{1,0:T(8,128)} copy(f32[48,1024]{1,0:T(8,128)} %get-tuple-element.13) | data formatting | bytes 393216

commit v2 on v1

v2 whole, which is shorter than its diff:
```python
import jax
import jax.numpy as jnp
from jax import lax
from jax.experimental import pallas as pl
from jax.experimental.pallas import tpu as pltpu
from jax.sharding import Mesh
from jax.sharding import PartitionSpec as P

MESH = pl.DeviceIdType.MESH
F32, BF16, I32 = jnp.float32, jnp.bfloat16, jnp.int32
NZ, NX, NY, NC = 8, 4, 4, 2
D, HID, TRAJ, SLOTS = 1536, 1024, 6, 12
UNITS, ROWS, CH = 12, 768, 192
KSTEPS = 10
SURV = 192
EPS = 1e-06
GELU_K = 0.7978845608028654
GELU_C = 0.044715


def tri(s):
    return lax.rem(s * s * s, 5)


def kernel(
    slot_s, src_s, cnt_s, rank_v, time_v, src_h, slot_h, lat_h, noi_h, old_h, wpatch_h, modl_h, wv_h, wup_h, wdn_h,
    out_up, out_dn, out_loss,
    src_v, slot_v, lat, noi, old, wpatch, modl, wv, dfin_s, wdn_t, meta, wup, wdn, snd_a, snd_b, rcv_a, rcv_b, meta_l, meta_all, meta_flat, tmp, xs, nz, od,
    mod_s, mod_c, mod_g, coef_u, adv_u, emb, modb, act, dg, dpre, dsend, drecv, pk, ysend, yrecv, pfull,
    fin, finb, inv, ups, mod_t, up_t, gu, gd, zr, xr, s2u, s2d, s2ur, s2dr, loss_own, loss_x, loss_z,
    up_v, dn_v, loss_v, lsem, osem, ssem, rsem,
):
    z, x, y, c = (lax.axis_index(n) for n in ("z", "x", "y", "c"))
    owner = z * NX + x

    def dev(dz=0, dx=0, dy=0, dc=0):
        return (
            lax.rem(z + (dz + NZ), NZ),
            lax.rem(x + (dx + NX), NX),
            lax.rem(y + (dy + NY), NY),
            lax.rem(c + dc, NC),
        )

    nxt = lax.rem(owner + 1, NZ * NX)
    prv = lax.rem(owner + NZ * NX - 1, NZ * NX)
    next_dev = (nxt // NX, lax.rem(nxt, NX), y, c)
    prev_dev = (prv // NX, lax.rem(prv, NX), y, c)

    ids = {}

    def mid(name):
        return ids.setdefault(name, len(ids))

    sent = []

    def copy(name, src, dst, to):
        i = mid(name) if isinstance(name, str) else name
        return pltpu.make_async_remote_copy(
            src_ref=src, dst_ref=dst, send_sem=ssem.at[i], recv_sem=rsem.at[i],
            device_id=to, device_id_type=MESH,
        )

    def send(name, src, dst, to):
        d = copy(name, src, dst, to)
        d.start()
        sent.append(d)

    def recv(name, dst, to=None):
        copy(name, dst, dst, dev(dc=1) if to is None else to).wait_recv()

    barrier = pltpu.get_barrier_semaphore()
    peers = [dev(dx=2), dev(dx=1), dev(dx=-1), dev(dz=1), dev(dz=-1), dev(dy=1), dev(dy=-1), dev(dc=1), next_dev, prev_dev]
    for p in peers:
        pl.semaphore_signal(barrier, inc=1, device_id=p, device_id_type=MESH)
    pairs = (
        (lat_h, lat), (noi_h, noi), (old_h, old), (modl_h, modl), (wpatch_h, wpatch), (wdn_h, wdn), (wup_h, wup), (wv_h, wv),
        (src_h, src_v), (slot_h, slot_v),
    )
    loads = [pltpu.make_async_copy(a, b, lsem.at[i]) for i, (a, b) in enumerate(pairs)]
    for cp in loads:
        cp.start()
    meta[0:1, 0:SLOTS] = rank_v[...]
    meta[1:3, 0:SLOTS] = time_v[...]
    meta_all[z * NX + x] = meta[...]
    lead_n = jnp.minimum(owner + 1, NZ * NX - 1) * TRAJ
    lead = owner * TRAJ
    next_slots = [slot_s[lead_n + i] for i in range(TRAJ)]
    loads[0].wait()
    for i in range(TRAJ):
        snd_a[i] = lat[next_slots[i]]
    pl.semaphore_wait(barrier, len(peers))
    send("meta_l", meta, meta_l, next_dev)
    send("shift_a", snd_a, rcv_a, next_dev)
    loads[1].wait()
    loads[2].wait()
    for i in range(TRAJ):
        snd_b[0, i] = noi[next_slots[i]]
        snd_b[1, i] = old[next_slots[i]]
    send("shift_b", snd_b, rcv_b, next_dev)
    row_of = lambda d: z * NX + lax.rem(x + (d + NX), NX)
    block = lambda d: pl.ds(lax.rem(z + (d + NZ), NZ) * NX, NX)
    for d in (1, -1):
        send(f"meta_x{d}", meta, meta_all.at[row_of(0)], dev(dx=d))

    def meta_step(n):
        if n == 0:
            recv("meta_x1", meta_all.at[row_of(-1)])
            recv("meta_x-1", meta_all.at[row_of(1)])
            copy("meta_xx", meta_all.at[row_of(-1)], meta_all.at[row_of(-1)], dev(dx=1)).start()
            return
        if n == 1:
            recv("meta_xx", meta_all.at[row_of(-2)])
        for d in (1, -1):
            if n > 1 and (d == 1 or n < 5):
                recv(f"meta_z{d}_{n - 1}", meta_all.at[block(-d * (n - 1))])
            if n < 4 or (n == 4 and d == 1):
                b = block(-d * (n - 1))
                copy(f"meta_z{d}_{n}", meta_all.at[b], meta_all.at[b], dev(dz=d)).start()

    def meta_sent():
        sent.append(copy("meta_xx", meta_all.at[row_of(-1)], meta_all.at[row_of(-1)], dev(dx=1)))
        for d, last in ((1, 4), (-1, 3)):
            for n in range(1, last + 1):
                b = block(-d * (n - 1))
                sent.append(copy(f"meta_z{d}_{n}", meta_all.at[b], meta_all.at[b], dev(dz=d)))

    loads[5].wait()
    for b in range(4):
        wdn_t[:, 384 * b : 384 * b + 384] = wdn[384 * b : 384 * b + 384, :].T
    loads[3].wait()

    slots = [slot_s[lead + i] for i in range(TRAJ)]
    lefts = [src_s[lead + i] != owner for i in range(TRAJ)]

    sub = lax.broadcasted_iota(I32, (16, 128), 0)
    lane = lax.broadcasted_iota(I32, (16, 128), 1)
    pos = jnp.zeros((16, 128), I32)
    from_left = jnp.zeros((16, 128), I32)
    for i in range(TRAJ):
        mine = (sub >> 1) == i
        pos = pos + jnp.where(mine, slots[i], 0)
        from_left = from_left + jnp.where(mine, lefts[i].astype(I32), 0)
    recv("meta_l", meta_l)

    def step_row(n):
        wide = [jnp.broadcast_to(m[n : n + 1, :], (16, 128)) for m in (meta_l, meta)]
        return jnp.where(from_left == 1, wide[0], wide[1])

    row = jnp.where((sub & 1) == 0, step_row(1), step_row(2))
    stamp = jnp.sum(jnp.where(lane == pos, row.astype(F32), 0.0), axis=1, keepdims=True)
    level = 1.0 - stamp * (1.0 / KSTEPS)
    coef = jnp.sqrt((1.0 / KSTEPS) * (1.0 - level + (1.0 / KSTEPS)) / level) / 0.7
    coef_u[...] = jnp.broadcast_to(coef, (16, 128))
    for kind, dst in ((0, mod_s), (1, mod_c), (2, mod_g)):
        acc = jnp.zeros((16, D), F32)
        for t in range(KSTEPS):
            acc = jnp.where(stamp == float(t), jnp.broadcast_to(modl[t, pl.ds(kind, 1), :], (16, D)), acc)
        dst[...] = acc + 1.0 if kind == 1 else acc

    def assemble(own, arrived, i):
        v = jnp.where(lefts[i], arrived.astype(F32), own.astype(F32))
        tmp[...] = v
        return tmp[pl.ds(0, 32, stride=2), :], tmp[pl.ds(1, 32, stride=2), :]

    recv("shift_a", rcv_a)
    for i in range(TRAJ):
        for step, v in enumerate(assemble(lat[slots[i]], rcv_a[i], i)):
            u = 2 * i + step
            xs[u // 3, (u % 3) * 32 : (u % 3) * 32 + 32, :] = v

    def spread(pair):
        return jnp.concatenate([pair[:, :64], pltpu.roll(pair, 64, 1)[:, :64]], axis=0)

    for i in (4, 6, 7, 8, 9):
        loads[i].wait()

    chunk_of = [lax.rem(y + i, NY) for i in (2, 3, 1, 0)]

    def embed(s):
        k, r0 = chunk_of[s], s * CH
        emb[r0 : r0 + CH, :] = jnp.dot(spread(xs[k]).astype(BF16), wpatch[...], preferred_element_type=F32)

    def norm(s, blocks):
        for b in blocks:
            rb = s * CH + b * 16
            u = chunk_of[s] * 3 + (b % 6) // 2
            v = emb[rb : rb + 16, :]
            v = v - jnp.mean(v, axis=-1, keepdims=True)
            i = lax.rsqrt(jnp.mean(v * v, axis=-1, keepdims=True) + EPS)
            modb[rb : rb + 16, :] = (v * i * mod_c[pl.ds(u, 1), :] + mod_s[pl.ds(u, 1), :]).astype(BF16)

    def up(s, n):
        rows, cols = slice(s * CH, s * CH + CH), slice(256 * n, 256 * n + 256)
        pre = jnp.dot(modb[rows, :], wup[:, cols], preferred_element_type=F32)
        sq = pre * pre
        th = jnp.tanh(GELU_K * (pre + GELU_C * (sq * pre)))
        half = 0.5 * (1.0 + th)
        act[rows, cols] = (pre * half).astype(BF16)
        dg[rows, cols] = half + (0.5 * GELU_K) * pre * (1.0 - th * th) * (1.0 + 3.0 * GELU_C * sq)

    def down(s):
        rows = slice(s * CH, s * CH + CH)
        for j in range(2):
            q = pl.multiple_of((1 - c if j == 0 else c) * 768, 768)
            v = jnp.dot(act[rows, :], wdn_t[:, pl.ds(q, 768)], preferred_element_type=F32)
            for h in range(2):
                if j == 0:
                    dsend[s, h] = v[:, 384 * h : 384 * h + 384].astype(BF16)
                else:
                    pk[s, h] = v[:, 384 * h : 384 * h + 384]
            if j == 0:
                send(f"d2d{s}", dsend.at[s], drecv.at[s], dev(dc=1))

    def presum(s):
        recv(f"d2d{s}", drecv.at[s])
        for h in range(2):
            pk[s, h] = pk[s, h] + drecv[s, h].astype(F32)

    def ygo(name, i, v, d):
        ysend[i] = v.astype(BF16)
        send(name, ysend.at[i], yrecv.at[i], dev(dy=d))

    def yphase(s):
        if s == 1:
            presum(0)
            ygo("y1a", 0, pk[0, 0], 1)
            ygo("y1b", 1, pk[0, 1], -1)
        elif s == 2:
            presum(1)
            ygo("y2a", 2, pk[1, 0], -1)
        elif s == 3:
            presum(2)
            ygo("y2b", 3, pk[2, 1], 1)

    embed(0)
    norm(0, range(12))
    for s in range(4):
        if s < 3:
            embed(s + 1)
        for n in range(4):
            up(s, n)
            if s < 3:
                norm(s + 1, range(3 * n, 3 * n + 3))
        yphase(s)
        down(s)
        meta_step(s)
    recv("y1a", yrecv.at[0])
    ygo("y3a", 5, pk[2, 0] + yrecv[0].astype(F32), 1)
    recv("y1b", yrecv.at[1])
    ygo("y3b", 4, pk[1, 1] + yrecv[1].astype(F32), -1)

    def transpose_pair(p, src, put):
        tok = slice(p * 384, p * 384 + 384)
        for b in range(4):
            put(b, tok, src[tok, 384 * b : 384 * b + 384].T)

    def put_up(b, tok, t):
        up_t[2 * b, :, tok] = t[:192]
        up_t[2 * b + 1, :, tok] = t[192:]

    def put_mod(b, tok, t):
        for zz in range(2):
            for xx in range(NX):
                o = zz * 192 + xx * 48
                mod_t[xx, (2 * b + zz) * 48 : (2 * b + zz) * 48 + 48, tok] = t[o : o + 48]

    presum(3)
    for p in range(2):
        transpose_pair(p, modb, put_mod)

    q0 = 2 * c
    recv("y2a", yrecv.at[2])
    recv("y3a", yrecv.at[5])
    pfull[y, q0] = (pk[3, 0] + yrecv[2].astype(F32) + yrecv[5].astype(F32)).astype(BF16)
    send("g_up_a", pfull.at[y, q0], pfull.at[y, q0], dev(dy=1))
    recv("y2b", yrecv.at[3])
    recv("y3b", yrecv.at[4])
    pfull[y, q0 + 1] = (pk[3, 1] + yrecv[3].astype(F32) + yrecv[4].astype(F32)).astype(BF16)
    send("g_dn_b", pfull.at[y, q0 + 1], pfull.at[y, q0 + 1], dev(dy=-1))
    send("g_up_b", pfull.at[y, q0 + 1], pfull.at[y, q0 + 1], dev(dy=1))
    send("g_dn_a", pfull.at[y, q0], pfull.at[y, q0], dev(dy=-1))
    send("c_own", pfull.at[y, pl.ds(q0, 2)], pfull.at[y, pl.ds(q0, 2)], dev(dc=1))

    meta_step(4)
    recv("shift_b", rcv_b)
    for i in range(TRAJ):
        for arr, which, dst in ((noi, 0, nz), (old, 1, od)):
            for step, v in enumerate(assemble(arr[slots[i]], rcv_b[which, i], i)):
                u = 2 * i + step
                dst[u // 3, (u % 3) * 32 : (u % 3) * 32 + 32, :] = v

    meta_step(5)
    meta_sent()
    for r in range(NZ * NX):
        meta_flat[r : r + 1, :] = meta_all[r, 0:1, :]
    ranks = meta_flat[...]
    hot = (lax.broadcasted_iota(I32, (NZ * NX, SURV), 0) == src_v[...]).astype(F32).astype(BF16)
    first = (((0,), (0,)), ((), ()))
    hi = lax.dot_general((ranks >> 4).astype(F32).astype(BF16), hot, first, preferred_element_type=F32)[:16]
    lo = lax.dot_general((ranks & 15).astype(F32).astype(BF16), hot, first, preferred_element_type=F32)[:16]
    by_slot = hi * 16.0 + lo
    rank = jnp.sum(
        jnp.where(lax.broadcasted_iota(I32, (16, SURV), 0) == slot_v[...], by_slot, 0.0), axis=0, keepdims=True
    )
    rank_i = rank.astype(I32)
    sq_i = rank_i * rank_i
    sq_hi, sq_lo = (sq_i >> 10).astype(F32), (sq_i & 1023).astype(F32)
    jdx = lax.broadcasted_iota(I32, (1, SURV), 1)

    def bounds(g, carry):
        end = carry[0] + cnt_s[g]
        out = [end]
        for i in range(TRAJ):
            hit = (lead + i >= carry[0]) & (lead + i < end)
            out += [jnp.where(hit, carry[0], carry[1 + 2 * i]), jnp.where(hit, end, carry[2 + 2 * i])]
        return tuple(out)

    ends = lax.fori_loop(0, 48, bounds, (jnp.int32(0),) * (1 + 2 * TRAJ))
    for i in range(TRAJ):
        lo_i, hi_i = ends[1 + 2 * i], ends[2 + 2 * i]
        inside = (jdx >= lo_i) & (jdx < hi_i)

        def total(v):
            return jnp.sum(jnp.where(inside, v, 0.0), axis=1, keepdims=True)

        s1 = total(rank)
        s1_i = s1.astype(I32)
        s2_i = total(sq_hi).astype(I32) * 1024 + total(sq_lo).astype(I32)
        n_i = jnp.full((1, 1), hi_i - lo_i, I32)
        n = n_i.astype(F32)
        r = jnp.sum(jnp.where(jdx == lead + i, rank, 0.0), axis=1, keepdims=True)
        dev_i = jnp.sqrt((n_i * s2_i - s1_i * s1_i).astype(F32)) / n
        a = (r - s1 / n) / jnp.maximum(dev_i, 1.0)
        adv_u[2 * i : 2 * i + 2, :] = jnp.broadcast_to(a, (2, 128))

    loss_own[...] = jnp.zeros((1, 128), F32)

    def head(k, r0, behind):

        def mix(t, carry):
            for b in range(6):
                o = pl.multiple_of(t * 96 + b * 16, 16)
                u = k * 3 + b // 2
                proj = jnp.concatenate([pfull[k, q, pl.ds(o, 16), :] for q in range(4)], axis=1).astype(F32)
                v = emb[pl.ds(pl.multiple_of(r0 + o, 16), 16), :] + mod_g[pl.ds(u, 1), :] * proj
                v = v - jnp.mean(v, axis=-1, keepdims=True)
                i = lax.rsqrt(jnp.mean(v * v, axis=-1, keepdims=True) + EPS)
                v = v * i
                fin[pl.ds(o, 16), :] = v
                finb[pl.ds(o, 16), :] = v.astype(BF16)
                inv[pl.ds(o, 16), :] = jnp.broadcast_to(i, (16, 128))
            if behind is not None:
                dact(behind, pl.multiple_of(t * 512, 512))
            return carry

        lax.fori_loop(0, 2, mix, 0)
        velocity = lax.dot_general(finb[...], wv[...], (((1,), (1,)), ((), ())), preferred_element_type=F32)
        drawn, target = spread(nz[k]), spread(od[k])
        err = velocity - target
        dv = [None] * 6
        for j in range(3):
            u = k * 3 + j
            cu = coef_u[pl.ds(u, 1), :][:, :64]
            au = adv_u[pl.ds(u, 1), :][:, :1]
            part = jnp.zeros((32, 64), F32)
            for h in range(2):
                o = h * 96 + j * 32
                e, n = err[o : o + 32], drawn[o : o + 32]
                part = part + cu * n * e + 0.5 * cu * cu * e * e
            logratio = -jnp.sum(jnp.sum(part, axis=0, keepdims=True), axis=1, keepdims=True) * (1.0 / 4096)
            ratio = jnp.exp(logratio)
            plain = ratio * au
            bounded = jnp.clip(ratio, 0.8, 1.2) * au
            loss_own[...] += jnp.broadcast_to(-jnp.minimum(plain, bounded), (1, 128))
            slope = jnp.where(plain <= bounded, -au * ratio * (1.0 / (SURV * 2)), 0.0)
            for h in range(2):
                o = h * 96 + j * 32
                e, n = err[o : o + 32], drawn[o : o + 32]
                dv[h * 3 + j] = slope * (-(cu * n + cu * cu * e) * (1.0 / 4096))
        dvel = jnp.concatenate(dv, axis=0).astype(BF16)
        dfin = jnp.dot(dvel, wv[...], preferred_element_type=F32)
        dfin_s[...] = dfin

        def back(t, carry):
            for b in range(6):
                o = pl.multiple_of(t * 96 + b * 16, 16)
                u = k * 3 + b // 2
                g = dfin_s[pl.ds(o, 16), :]
                f = fin[pl.ds(o, 16), :]
                m1 = jnp.mean(g, axis=-1, keepdims=True)
                m2 = jnp.mean(g * f, axis=-1, keepdims=True)
                i = inv[pl.ds(o, 16), :][:, :1]
                ups[pl.ds(pl.multiple_of(r0 + o, 16), 16), :] = (
                    mod_g[pl.ds(u, 1), :] * (i * (g - m1 - f * m2))
                ).astype(BF16)
            return carry

        lax.fori_loop(0, 2, back, 0)

    def dact(r0, lo):
        rows, cols = slice(r0, r0 + CH), pl.ds(lo, 512)
        v = jnp.dot(ups[rows, :], wdn[:, cols], preferred_element_type=F32)
        dpre[rows, cols] = (v * dg[rows, cols]).astype(BF16)

    yu, yd, yo = (lax.rem(y + i, NY) for i in (1, 3, 2))
    p0 = 2 - 2 * c

    def fwd_core(name, k, q):
        send(name, pfull.at[k, q], pfull.at[k, q], dev(dc=1))

    def got(name, k, q):
        recv(name, pfull.at[k, q])

    recv("c_own", pfull.at[y, pl.ds(p0, 2)])
    head(y, 3 * CH, None)
    got("g_up_a", yd, q0)
    send("r_up", pfull.at[yd, q0], pfull.at[yd, q0], dev(dy=1))
    fwd_core("c_da", yd, q0)
    got("g_dn_b", yu, q0 + 1)
    send("r_dn", pfull.at[yu, q0 + 1], pfull.at[yu, q0 + 1], dev(dy=-1))
    fwd_core("c_ub", yu, q0 + 1)
    got("g_dn_a", yu, q0)
    fwd_core("c_ua", yu, q0)
    got("g_up_b", yd, q0 + 1)
    fwd_core("c_db", yd, q0 + 1)
    got("c_ua", yu, p0)
    got("c_ub", yu, p0 + 1)
    head(yu, 2 * CH, 3 * CH)
    got("r_up", yo, q0)
    fwd_core("c_oa", yo, q0)
    got("r_dn", yo, q0 + 1)
    fwd_core("c_ob", yo, q0 + 1)
    got("c_da", yd, p0)
    got("c_db", yd, p0 + 1)
    head(yd, CH, 2 * CH)
    transpose_pair(1, ups, put_up)
    got("c_oa", yo, p0)
    got("c_ob", yo, p0 + 1)
    head(yo, 0, CH)
    transpose_pair(0, ups, put_up)

    def grad_x(off):
        k = at(x, NX, off)
        for h in range(2):
            v = jnp.dot(mod_t[k], dpre[:, 512 * h : 512 * h + 512], preferred_element_type=F32).astype(BF16)
            gd[k, 2 * h], gd[k, 2 * h + 1] = v[:, :256], v[:, 256:]

    def grad_z(off):
        k = at(z, NZ, off)
        for h in range(2):
            v = jnp.dot(up_t[k], act[:, 512 * h : 512 * h + 512], preferred_element_type=F32).astype(BF16)
            gu[k, 2 * h], gu[k, 2 * h + 1] = v[:, :256], v[:, 256:]

    def at(axis_pos, n, off):
        return lax.rem(axis_pos + (off + n), n)

    def ring(n):
        spec = {}
        for d in (1, -1):
            for h in range(2):
                far = (h == 0) == (d == 1)
                last = n // 2 if far else n // 2 - 1
                for i in range(1, last + 1):
                    spec[d, h, i] = (d * (last + 1 - i), h, d)
        return spec, {m: i for i, m in enumerate(spec)}

    zspec, zi = ring(NZ)
    xspec, xi = ring(NX)

    class Stream:
        def __init__(self, tag, axis, buf, land):
            self.tag, self.axis, self.buf, self.land = tag, axis, buf, land
            self.spec, self.idx = (zspec, zi) if axis == "z" else (xspec, xi)
            self.pos, self.n = (z, NZ) if axis == "z" else (x, NX)

        def slot(self, b, m):
            return self.land.at[b * len(self.spec) + self.idx[m]]

        def go(self, b, *m):
            off, h, d = self.spec[m]
            to = dev(dz=d) if self.axis == "z" else dev(dx=d)
            send(f"{self.tag}{b}{m}", self.buf.at[at(self.pos, self.n, off), 2 * b + h], self.slot(b, m), to)

        def got(self, b, m):
            recv(f"{self.tag}{b}{m}", self.slot(b, m))
            return self.land[b * len(self.spec) + self.idx[m]].astype(F32)

        def relay(self, b, d, h, i):
            off = self.spec[d, h, i][0]
            k = at(self.pos, self.n, off)
            v = self.got(b, (d, h, i - 1))
            self.buf[k, 2 * b + h] = (self.buf[k, 2 * b + h].astype(F32) + v).astype(BF16)
            self.go(b, d, h, i)

        def far(self, b, i):
            self.relay(b, 1, 0, i)
            self.relay(b, -1, 1, i)

        def near(self, b, i):
            self.relay(b, 1, 1, i)
            self.relay(b, -1, 0, i)

        def total(self, b, h):
            v = self.buf[at(self.pos, self.n, 0), 2 * b + h].astype(F32)
            for d in (1, -1):
                last = max(i for e, g, i in self.spec if (e, g) == (d, h))
                v = v + self.got(b, (d, h, last))
            return v

        def first(self, b):
            self.go(b, 1, 0, 1)
            self.go(b, -1, 1, 1)

    Z1 = Stream("z", "z", gu, zr)
    X1 = Stream("x", "x", gd, xr)
    X2 = Stream("s", "z", s2d, s2dr)

    def finish_x(b):
        for h in range(2):
            v = X1.total(b, h).astype(BF16)
            for i in range(NZ):
                s2d[i, 2 * b + h] = v[48 * i : 48 * i + 48]
        X2.first(b)
        X2.go(b, 1, 1, 1)
        X2.go(b, -1, 0, 1)

    def hop(b, i):
        X2.far(b, i)
        if i < 4:
            X2.near(b, i)

    def done_x(b):
        for h in range(2):
            up_v[b, :, 256 * h : 256 * h + 256] = X2.total(b, h)
        store(f"up{b}", up_v.at[b], out_up.at[:, pl.ds(512 * b, 512)])

    def finish_z(b):
        for h in range(2):
            v = Z1.total(b, h).astype(BF16)
            for i in range(NX):
                s2u[b, i, :, 256 * h : 256 * h + 256] = v[48 * i : 48 * i + 48]
        for i in (2, 1, 3):
            send(f"t{b}{i}", s2u.at[b, at(x, NX, i)], s2ur.at[b, i], dev(dx=i))

    def done_z(b):
        v = s2u[b, x].astype(F32)
        for i in (1, 3, 2):
            recv(f"t{b}{i}", s2ur.at[b, i])
            v = v + s2ur[b, i].astype(F32)
        dn_v[b] = v
        store(f"dn{b}", dn_v.at[b], out_dn.at[:, pl.ds(512 * b, 512)])

    stores = []

    def store(name, src, dst):
        d = pltpu.make_async_copy(src, dst, osem.at[len(stores)])
        d.start()
        stores.append(d)

    def loss_step(n):
        if n == 0:
            for d in (1, -1):
                send(f"loss_x{d}", loss_own, loss_x.at[d % 4], dev(dx=d))
        elif n == 1:
            recv("loss_x1", loss_x.at[1])
            recv("loss_x-1", loss_x.at[3])
            send("loss_xx", loss_x.at[1], loss_x.at[2], dev(dx=1))
        elif n == 2:
            recv("loss_xx", loss_x.at[2])
            loss_z[0] = loss_own[...] + loss_x[1] + loss_x[2] + loss_x[3]
        if n >= 2:
            for d in (1, -1):
                if n > 2 and (d == 1 or n < 6):
                    recv(f"loss_z{d}_{n - 1}", loss_z.at[(d * (n - 2)) % NZ])
                if n < 5 or (n == 5 and d == 1):
                    send(f"loss_z{d}_{n}", loss_z.at[(d * (n - 2)) % NZ], loss_z.at[(d * (n - 1)) % NZ], dev(dz=d))

    grad_z(4)
    Z1.first(0)
    grad_z(3)
    Z1.go(0, 1, 1, 1)
    grad_z(-3)
    Z1.go(0, -1, 0, 1)
    for lo in (0, 512):
        dact(0, lo)
    grad_x(2)
    X1.first(0)
    Z1.first(1)
    loss_step(0)
    grad_x(-1)
    X1.go(0, -1, 0, 1)
    grad_x(1)
    X1.go(0, 1, 1, 1)
    Z1.far(0, 2)
    loss_step(1)
    grad_z(2)
    grad_z(-2)
    Z1.go(1, 1, 1, 1)
    Z1.go(1, -1, 0, 1)
    Z1.near(0, 2)
    X1.far(0, 2)
    grad_z(1)
    grad_z(-1)
    X1.first(1)
    loss_step(2)
    Z1.far(0, 3)
    grad_z(0)
    grad_x(0)
    Z1.far(1, 2)
    X1.go(1, 1, 1, 1)
    X1.go(1, -1, 0, 1)
    Z1.near(0, 3)
    loss_step(3)
    Z1.near(1, 2)
    Z1.far(0, 4)
    finish_x(0)
    X1.far(1, 2)
    loss_step(4)
    Z1.far(1, 3)
    hop(0, 2)
    finish_z(0)
    Z1.near(1, 3)
    loss_step(5)
    hop(0, 3)
    Z1.far(1, 4)
    finish_x(1)
    hop(0, 4)
    loss_step(6)
    v = loss_z[0]
    for i in range(1, NZ):
        v = v + loss_z[i]
    loss_v[...] = v * (1.0 / (SURV * 2))
    store("loss", loss_v, out_loss)
    hop(1, 2)
    done_x(0)
    done_z(0)
    finish_z(1)
    hop(1, 3)
    hop(1, 4)
    done_z(1)
    done_x(1)
    for d in stores:
        d.wait()
    for d in sent:
        d.wait_send()
    assert len(ids) <= NSEM, len(ids)


NSEM = 136


def shards(
    latents, noise, behavior_velocity, timestep, reward_rank_integer, surviving_source_index,
    surviving_slot_index, group_kept_count, patch_input_weight, modulation_lookup,
    up_projection_weight, down_projection_weight, velocity_head_weight,
):
    def pairs(a):
        return a.reshape(SLOTS, 2, 32, 128).transpose(0, 2, 1, 3).reshape(SLOTS, 64, 128)

    smem = pl.BlockSpec(memory_space=pltpu.SMEM)
    vmem = pl.BlockSpec(memory_space=pltpu.VMEM)
    hbm = pl.BlockSpec(memory_space=pl.ANY)
    V = pltpu.VMEM
    piece = (CH, 384)
    scratch = [
        V((1, SURV), I32), V((1, SURV), I32),
        V((SLOTS, 64, 128), BF16), V((SLOTS, 64, 128), BF16), V((SLOTS, 64, 128), BF16), V((64, D), BF16),
        V((KSTEPS, 3, D), F32), V((64, D), BF16), V((CH, D), F32), V((HID, D), BF16),
        V((8, 128), I32), V((D, HID), BF16), V((D, HID), BF16),
        V((TRAJ, 64, 128), BF16), V((2, TRAJ, 64, 128), BF16), V((TRAJ, 64, 128), BF16), V((2, TRAJ, 64, 128), BF16),
        V((8, 128), I32), V((NZ * NX, 8, 128), I32), V((NZ * NX, 128), I32), V((64, 128), F32),
        V((4, 96, 128), F32), V((4, 96, 128), F32), V((4, 96, 128), F32),
        V((16, D), F32), V((16, D), F32), V((16, D), F32), V((16, 128), F32), V((16, 128), F32),
        V((ROWS, D), F32), V((ROWS, D), BF16), V((ROWS, HID), BF16), V((ROWS, HID), F32), V((ROWS, HID), BF16),
        V((4, 2, *piece), BF16), V((4, 2, *piece), BF16), V((4, 2, *piece), F32),
        V((6, *piece), BF16), V((6, *piece), BF16), V((4, 4, *piece), BF16),
        V((CH, D), F32), V((CH, D), BF16), V((CH, 128), F32), V((ROWS, D), BF16),
        V((NX, 384, ROWS), BF16), V((NZ, 192, ROWS), BF16),
        V((NZ, 4, 192, 256), BF16), V((NX, 4, 384, 256), BF16), V((28, 192, 256), BF16), V((12, 384, 256), BF16),
        V((2, NX, 48, 512), BF16), V((NZ, 4, 48, 256), BF16), V((2, NX, 48, 512), BF16), V((28, 48, 256), BF16),
        V((1, 128), F32), V((NX, 1, 128), F32), V((NZ, 1, 128), F32),
        V((2, 48, 512), F32), V((2, 48, 512), F32), V((1, 128), F32),
        pltpu.SemaphoreType.DMA((10,)), pltpu.SemaphoreType.DMA((5,)), pltpu.SemaphoreType.DMA((NSEM,)), pltpu.SemaphoreType.DMA((NSEM,)),
    ]
    up, dn, loss = pl.pallas_call(
        kernel,
        out_shape=(
            jax.ShapeDtypeStruct((48, HID), F32),
            jax.ShapeDtypeStruct((48, HID), F32),
            jax.ShapeDtypeStruct((1, 128), F32),
        ),
        in_specs=[smem] * 3 + [vmem] * 2 + [hbm] * 10,
        out_specs=(hbm,) * 3,
        scratch_shapes=scratch,
        compiler_params=pltpu.CompilerParams(collective_id=0, has_side_effects=True, vmem_limit_bytes=67043328),
    )(
        surviving_slot_index, surviving_source_index, group_kept_count,
        reward_rank_integer.reshape(1, SLOTS), timestep.T,
        surviving_source_index.reshape(1, SURV), surviving_slot_index.reshape(1, SURV), pairs(latents), pairs(noise), pairs(behavior_velocity),
        patch_input_weight, modulation_lookup, velocity_head_weight.T,
        up_projection_weight, down_projection_weight,
    )
    return up, dn, loss[0, 0]


def solution(mesh):
    finer = Mesh(mesh.devices.reshape(NZ, NX, NY, NC), ("z", "x", "y", "c"))
    dp, fs = ("z", "x"), ("y", "c")
    in_specs = (
        P(dp, None, None), P(dp, None, None), P(dp, None, None), P(dp, None), P(dp), P(), P(), P(), P(), P(),
        P(None, fs), P(None, fs), P(),
    )
    out_specs = (P(dp, fs), P(dp, fs), P())
    return jax.shard_map(shards, mesh=finer, in_specs=in_specs, out_specs=out_specs, check_vma=False)
```

time: 122 us -> 107 us (0.88)
  Pallas kernels: 116 us -> 101 us
    pallas_call x1, Pallas kernels: 116 us -> 101 us  [shards(): pl.pallas_call(kernel, out_shape=(jax.ShapeDtypeStruct((48, HID), F32), j...]
where the time goes in v2:
time: 107 us
  Pallas kernels  101 us (94%)
  local copies, waits for them, and re-layouts  3.23 us (3%)
  between operations  2.4 us (2%)
    pallas_call x1, Pallas kernels, shards(): pl.pallas_call(kernel, out_shape=(jax.ShapeDtypeStruct((48, HID), F32), j...  101 us
    unnamed x2, local copies, waits for them, and re-layouts  3.23 us

profile of v2, /device:TPU:32, one launch (start us, length us, event | category | flops | bytes accessed | tf_op | source)
XLA Modules:
  0.0 106.5 jit_solution(8854673478638928635)
XLA Ops:
  0.6 100.9 %shard_map.148 = (f32[48,1024]{1,0:T(8,128)}, f32[48,1024]{1,0:T(8,128)}, f32[1,128]{1,0:T(1,128)}) custom-call(s32[192]{0:T(256)} %slot_s.1, s32[192]{0:T(256)} %src_s.1, s32[48]{0:T(128)} %cnt_s.1, s32[1,12]{1,0:T(1,128)} %bitcast.29, s32[2,12]{1,0:T(2,128)} %bitcast.28, s32[1,192]{1,0:T(1,128)} %bitcast.27, s32[1,192]{1,0:T(1,128)} %bitcast.26, ...), custom_call_target="tpu_custom_call" | custom-call | tf_op jit(solution)/shard_map/pallas_call | solution.py:685
  101.6 1.6 %copy.22 = f32[48,1024]{1,0:T(8,128)} copy(f32[48,1024]{1,0:T(8,128)} %get-tuple-element.12) | data formatting | bytes 393216
  103.2 1.6 %copy.23 = f32[48,1024]{1,0:T(8,128)} copy(f32[48,1024]{1,0:T(8,128)} %get-tuple-element.13) | data formatting | bytes 393216

commit v3 on v2

--- a/solution.py
+++ b/solution.py
@@ -174,16 +174,18 @@
     for i in (4, 6, 7, 8, 9):
         loads[i].wait()
 
-    chunk_of = [lax.rem(y + i, NY) for i in (2, 3, 1, 0)]
+    yu, yd, yo = (lax.rem(y + i, NY) for i in (1, 3, 2))
+    held = ((yo, yo), (yd, yu), (yu, yd), (y, y))
 
     def embed(s):
-        k, r0 = chunk_of[s], s * CH
-        emb[r0 : r0 + CH, :] = jnp.dot(spread(xs[k]).astype(BF16), wpatch[...], preferred_element_type=F32)
+        even, odd = (xs[k] for k in held[s])
+        rows = jnp.concatenate([even[:, :64], pltpu.roll(odd, 64, 1)[:, :64]], axis=0)
+        emb[s * CH : s * CH + CH, :] = jnp.dot(rows.astype(BF16), wpatch[...], preferred_element_type=F32)
 
     def norm(s, blocks):
         for b in blocks:
             rb = s * CH + b * 16
-            u = chunk_of[s] * 3 + (b % 6) // 2
+            u = held[s][b // 6] * 3 + (b % 6) // 2
             v = emb[rb : rb + 16, :]
             v = v - jnp.mean(v, axis=-1, keepdims=True)
             i = lax.rsqrt(jnp.mean(v * v, axis=-1, keepdims=True) + EPS)
@@ -205,9 +207,9 @@
             v = jnp.dot(act[rows, :], wdn_t[:, pl.ds(q, 768)], preferred_element_type=F32)
             for h in range(2):
                 if j == 0:
-                    dsend[s, h] = v[:, 384 * h : 384 * h + 384].astype(BF16)
+                    dsend[s, h] = v[96 * h : 96 * h + 96].astype(BF16)
                 else:
-                    pk[s, h] = v[:, 384 * h : 384 * h + 384]
+                    pk[s, h] = v[96 * h : 96 * h + 96]
             if j == 0:
                 send(f"d2d{s}", dsend.at[s], drecv.at[s], dev(dc=1))
 
@@ -228,9 +230,13 @@
         elif s == 2:
             presum(1)
             ygo("y2a", 2, pk[1, 0], -1)
+            ygo("y2b", 3, pk[1, 1], 1)
         elif s == 3:
             presum(2)
-            ygo("y2b", 3, pk[2, 1], 1)
+            recv("y1a", yrecv.at[0])
+            ygo("y3a", 5, pk[2, 0] + yrecv[0].astype(F32), 1)
+            recv("y1b", yrecv.at[1])
+            ygo("y3b", 4, pk[2, 1] + yrecv[1].astype(F32), -1)
 
     embed(0)
     norm(0, range(12))
@@ -244,11 +250,6 @@
         yphase(s)
         down(s)
         meta_step(s)
-    recv("y1a", yrecv.at[0])
-    ygo("y3a", 5, pk[2, 0] + yrecv[0].astype(F32), 1)
-    recv("y1b", yrecv.at[1])
-    ygo("y3b", 4, pk[1, 1] + yrecv[1].astype(F32), -1)
-
     def transpose_pair(p, src, put):
         tok = slice(p * 384, p * 384 + 384)
         for b in range(4):
@@ -268,93 +269,38 @@
     for p in range(2):
         transpose_pair(p, modb, put_mod)
 
-    q0 = 2 * c
+    part = lambda k, h: pfull.at[k, c, h]
     recv("y2a", yrecv.at[2])
     recv("y3a", yrecv.at[5])
-    pfull[y, q0] = (pk[3, 0] + yrecv[2].astype(F32) + yrecv[5].astype(F32)).astype(BF16)
-    send("g_up_a", pfull.at[y, q0], pfull.at[y, q0], dev(dy=1))
+    pfull[y, c, 0] = (pk[3, 0] + yrecv[2].astype(F32) + yrecv[5].astype(F32)).astype(BF16)
+    send("g_up_a", part(y, 0), part(y, 0), dev(dy=1))
     recv("y2b", yrecv.at[3])
     recv("y3b", yrecv.at[4])
-    pfull[y, q0 + 1] = (pk[3, 1] + yrecv[3].astype(F32) + yrecv[4].astype(F32)).astype(BF16)
-    send("g_dn_b", pfull.at[y, q0 + 1], pfull.at[y, q0 + 1], dev(dy=-1))
-    send("g_up_b", pfull.at[y, q0 + 1], pfull.at[y, q0 + 1], dev(dy=1))
-    send("g_dn_a", pfull.at[y, q0], pfull.at[y, q0], dev(dy=-1))
-    send("c_own", pfull.at[y, pl.ds(q0, 2)], pfull.at[y, pl.ds(q0, 2)], dev(dc=1))
-
-    meta_step(4)
-    recv("shift_b", rcv_b)
-    for i in range(TRAJ):
-        for arr, which, dst in ((noi, 0, nz), (old, 1, od)):
-            for step, v in enumerate(assemble(arr[slots[i]], rcv_b[which, i], i)):
-                u = 2 * i + step
-                dst[u // 3, (u % 3) * 32 : (u % 3) * 32 + 32, :] = v
-
-    meta_step(5)
-    meta_sent()
-    for r in range(NZ * NX):
-        meta_flat[r : r + 1, :] = meta_all[r, 0:1, :]
-    ranks = meta_flat[...]
-    hot = (lax.broadcasted_iota(I32, (NZ * NX, SURV), 0) == src_v[...]).astype(F32).astype(BF16)
-    first = (((0,), (0,)), ((), ()))
-    hi = lax.dot_general((ranks >> 4).astype(F32).astype(BF16), hot, first, preferred_element_type=F32)[:16]
-    lo = lax.dot_general((ranks & 15).astype(F32).astype(BF16), hot, first, preferred_element_type=F32)[:16]
-    by_slot = hi * 16.0 + lo
-    rank = jnp.sum(
-        jnp.where(lax.broadcasted_iota(I32, (16, SURV), 0) == slot_v[...], by_slot, 0.0), axis=0, keepdims=True
-    )
-    rank_i = rank.astype(I32)
-    sq_i = rank_i * rank_i
-    sq_hi, sq_lo = (sq_i >> 10).astype(F32), (sq_i & 1023).astype(F32)
-    jdx = lax.broadcasted_iota(I32, (1, SURV), 1)
-
-    def bounds(g, carry):
-        end = carry[0] + cnt_s[g]
-        out = [end]
-        for i in range(TRAJ):
-            hit = (lead + i >= carry[0]) & (lead + i < end)
-            out += [jnp.where(hit, carry[0], carry[1 + 2 * i]), jnp.where(hit, end, carry[2 + 2 * i])]
-        return tuple(out)
-
-    ends = lax.fori_loop(0, 48, bounds, (jnp.int32(0),) * (1 + 2 * TRAJ))
-    for i in range(TRAJ):
-        lo_i, hi_i = ends[1 + 2 * i], ends[2 + 2 * i]
-        inside = (jdx >= lo_i) & (jdx < hi_i)
-
-        def total(v):
-            return jnp.sum(jnp.where(inside, v, 0.0), axis=1, keepdims=True)
-
-        s1 = total(rank)
-        s1_i = s1.astype(I32)
-        s2_i = total(sq_hi).astype(I32) * 1024 + total(sq_lo).astype(I32)
-        n_i = jnp.full((1, 1), hi_i - lo_i, I32)
-        n = n_i.astype(F32)
-        r = jnp.sum(jnp.where(jdx == lead + i, rank, 0.0), axis=1, keepdims=True)
-        dev_i = jnp.sqrt((n_i * s2_i - s1_i * s1_i).astype(F32)) / n
-        a = (r - s1 / n) / jnp.maximum(dev_i, 1.0)
-        adv_u[2 * i : 2 * i + 2, :] = jnp.broadcast_to(a, (2, 128))
+    pfull[y, c, 1] = (pk[3, 1] + yrecv[3].astype(F32) + yrecv[4].astype(F32)).astype(BF16)
+    send("g_dn_b", part(y, 1), part(y, 1), dev(dy=-1))
+    send("g_up_b", part(y, 1), part(y, 1), dev(dy=1))
+    send("g_dn_a", part(y, 0), part(y, 0), dev(dy=-1))
+    send("c_own", pfull.at[y, c], pfull.at[y, c], dev(dc=1))
 
     loss_own[...] = jnp.zeros((1, 128), F32)
 
-    def head(k, r0, behind):
-
-        def mix(t, carry):
-            for b in range(6):
-                o = pl.multiple_of(t * 96 + b * 16, 16)
-                u = k * 3 + b // 2
-                proj = jnp.concatenate([pfull[k, q, pl.ds(o, 16), :] for q in range(4)], axis=1).astype(F32)
-                v = emb[pl.ds(pl.multiple_of(r0 + o, 16), 16), :] + mod_g[pl.ds(u, 1), :] * proj
-                v = v - jnp.mean(v, axis=-1, keepdims=True)
-                i = lax.rsqrt(jnp.mean(v * v, axis=-1, keepdims=True) + EPS)
-                v = v * i
-                fin[pl.ds(o, 16), :] = v
-                finb[pl.ds(o, 16), :] = v.astype(BF16)
-                inv[pl.ds(o, 16), :] = jnp.broadcast_to(i, (16, 128))
-            if behind is not None:
-                dact(behind, pl.multiple_of(t * 512, 512))
-            return carry
-
-        lax.fori_loop(0, 2, mix, 0)
-        velocity = lax.dot_general(finb[...], wv[...], (((1,), (1,)), ((), ())), preferred_element_type=F32)
+    def mix(w, k, t, r0, behind=()):
+        for b in range(6):
+            o = t * 96 + b * 16
+            u = k * 3 + b // 2
+            proj = jnp.concatenate([pfull[k, q, t, b * 16 : b * 16 + 16, :] for q in range(2)], axis=1).astype(F32)
+            v = emb[r0 + b * 16 : r0 + b * 16 + 16, :] + mod_g[pl.ds(u, 1), :] * proj
+            v = v - jnp.mean(v, axis=-1, keepdims=True)
+            i = lax.rsqrt(jnp.mean(v * v, axis=-1, keepdims=True) + EPS)
+            v = v * i
+            fin[w, o : o + 16, :] = v
+            finb[w, o : o + 16, :] = v.astype(BF16)
+            inv[w, o : o + 16, :] = jnp.broadcast_to(i, (16, 128))
+        for slot, lo in behind:
+            dact(slot * CH, lo)
+
+    def rest(w, k, offs):
+        velocity = lax.dot_general(finb[w], wv[...], (((1,), (1,)), ((), ())), preferred_element_type=F32)
         drawn, target = spread(nz[k]), spread(od[k])
         err = velocity - target
         dv = [None] * 6
@@ -381,62 +327,119 @@
         dfin = jnp.dot(dvel, wv[...], preferred_element_type=F32)
         dfin_s[...] = dfin
 
-        def back(t, carry):
+        for t in range(2):
             for b in range(6):
-                o = pl.multiple_of(t * 96 + b * 16, 16)
+                o = t * 96 + b * 16
                 u = k * 3 + b // 2
-                g = dfin_s[pl.ds(o, 16), :]
-                f = fin[pl.ds(o, 16), :]
+                g = dfin_s[o : o + 16, :]
+                f = fin[w, o : o + 16, :]
                 m1 = jnp.mean(g, axis=-1, keepdims=True)
                 m2 = jnp.mean(g * f, axis=-1, keepdims=True)
-                i = inv[pl.ds(o, 16), :][:, :1]
-                ups[pl.ds(pl.multiple_of(r0 + o, 16), 16), :] = (
-                    mod_g[pl.ds(u, 1), :] * (i * (g - m1 - f * m2))
-                ).astype(BF16)
-            return carry
-
-        lax.fori_loop(0, 2, back, 0)
+                i = inv[w, o : o + 16, :][:, :1]
+                r = offs[t] + b * 16
+                ups[r : r + 16, :] = (mod_g[pl.ds(u, 1), :] * (i * (g - m1 - f * m2))).astype(BF16)
 
     def dact(r0, lo):
-        rows, cols = slice(r0, r0 + CH), pl.ds(lo, 512)
+        rows, cols = slice(r0, r0 + CH), slice(lo, lo + 512)
         v = jnp.dot(ups[rows, :], wdn[:, cols], preferred_element_type=F32)
         dpre[rows, cols] = (v * dg[rows, cols]).astype(BF16)
 
-    yu, yd, yo = (lax.rem(y + i, NY) for i in (1, 3, 2))
-    p0 = 2 - 2 * c
-
-    def fwd_core(name, k, q):
-        send(name, pfull.at[k, q], pfull.at[k, q], dev(dc=1))
-
-    def got(name, k, q):
-        recv(name, pfull.at[k, q])
-
-    recv("c_own", pfull.at[y, pl.ds(p0, 2)])
-    head(y, 3 * CH, None)
-    got("g_up_a", yd, q0)
-    send("r_up", pfull.at[yd, q0], pfull.at[yd, q0], dev(dy=1))
-    fwd_core("c_da", yd, q0)
-    got("g_dn_b", yu, q0 + 1)
-    send("r_dn", pfull.at[yu, q0 + 1], pfull.at[yu, q0 + 1], dev(dy=-1))
-    fwd_core("c_ub", yu, q0 + 1)
-    got("g_dn_a", yu, q0)
-    fwd_core("c_ua", yu, q0)
-    got("g_up_b", yd, q0 + 1)
-    fwd_core("c_db", yd, q0 + 1)
-    got("c_ua", yu, p0)
-    got("c_ub", yu, p0 + 1)
-    head(yu, 2 * CH, 3 * CH)
-    got("r_up", yo, q0)
-    fwd_core("c_oa", yo, q0)
-    got("r_dn", yo, q0 + 1)
-    fwd_core("c_ob", yo, q0 + 1)
-    got("c_da", yd, p0)
-    got("c_db", yd, p0 + 1)
-    head(yd, CH, 2 * CH)
+    def fwd_core(name, k, h):
+        send(name, part(k, h), part(k, h), dev(dc=1))
+
+    def got(name, k, h):
+        recv(name, part(k, h))
+
+    def core(name, k, h):
+        recv(name, pfull.at[k, 1 - c, h])
+
+    recv("shift_b", rcv_b)
+    for i in range(TRAJ):
+        for arr, which, dst in ((noi, 0, nz), (old, 1, od)):
+            for step, v in enumerate(assemble(arr[slots[i]], rcv_b[which, i], i)):
+                u = 2 * i + step
+                dst[u // 3, (u % 3) * 32 : (u % 3) * 32 + 32, :] = v
+
+    recv("c_own", pfull.at[y, 1 - c])
+    own = (3 * CH, 3 * CH + 96)
+    for t in range(2):
+        mix(0, y, t, own[t])
+    meta_step(4)
+    meta_step(5)
+    meta_sent()
+    for r in range(NZ * NX):
+        meta_flat[r : r + 1, :] = meta_all[r, 0:1, :]
+    ranks = meta_flat[...]
+    hot = (lax.broadcasted_iota(I32, (NZ * NX, SURV), 0) == src_v[...]).astype(F32).astype(BF16)
+    first = (((0,), (0,)), ((), ()))
+    hi = lax.dot_general((ranks >> 4).astype(F32).astype(BF16), hot, first, preferred_element_type=F32)[:16]
+    lo = lax.dot_general((ranks & 15).astype(F32).astype(BF16), hot, first, preferred_element_type=F32)[:16]
+    by_slot = hi * 16.0 + lo
+    rank = jnp.sum(
+        jnp.where(lax.broadcasted_iota(I32, (16, SURV), 0) == slot_v[...], by_slot, 0.0), axis=0, keepdims=True
+    )
+    rank_i = rank.astype(I32)
+    sq_i = rank_i * rank_i
+    sq_hi, sq_lo = (sq_i >> 10).astype(F32), (sq_i & 1023).astype(F32)
+    jdx = lax.broadcasted_iota(I32, (1, SURV), 1)
+
+    def bounds(g, carry):
+        end = carry[0] + cnt_s[g]
+        out = [end]
+        for i in range(TRAJ):
+            hit = (lead + i >= carry[0]) & (lead + i < end)
+            out += [jnp.where(hit, carry[0], carry[1 + 2 * i]), jnp.where(hit, end, carry[2 + 2 * i])]
+        return tuple(out)
+
+    ends = lax.fori_loop(0, 48, bounds, (jnp.int32(0),) * (1 + 2 * TRAJ))
+    for i in range(TRAJ):
+        lo_i, hi_i = ends[1 + 2 * i], ends[2 + 2 * i]
+        inside = (jdx >= lo_i) & (jdx < hi_i)
+
+        def total(v):
+            return jnp.sum(jnp.where(inside, v, 0.0), axis=1, keepdims=True)
+
+        s1 = total(rank)
+        s1_i = s1.astype(I32)
+        s2_i = total(sq_hi).astype(I32) * 1024 + total(sq_lo).astype(I32)
+        n_i = jnp.full((1, 1), hi_i - lo_i, I32)
+        n = n_i.astype(F32)
+        r = jnp.sum(jnp.where(jdx == lead + i, rank, 0.0), axis=1, keepdims=True)
+        dev_i = jnp.sqrt((n_i * s2_i - s1_i * s1_i).astype(F32)) / n
+        a = (r - s1 / n) / jnp.maximum(dev_i, 1.0)
+        adv_u[2 * i : 2 * i + 2, :] = jnp.broadcast_to(a, (2, 128))
+
+    rest(0, y, own)
+    got("g_up_a", yd, 0)
+    send("r_up", part(yd, 0), part(yd, 0), dev(dy=1))
+    fwd_core("c_da", yd, 0)
+    got("g_dn_b", yu, 1)
+    send("r_dn", part(yu, 1), part(yu, 1), dev(dy=-1))
+    fwd_core("c_ub", yu, 1)
+    core("c_da", yd, 0)
+    core("c_ub", yu, 1)
+    mix(0, yu, 1, CH + 96, [(3, 0)])
+    mix(1, yd, 0, CH, [(3, 512)])
+    got("g_dn_a", yu, 0)
+    fwd_core("c_ua", yu, 0)
+    got("g_up_b", yd, 1)
+    fwd_core("c_db", yd, 1)
+    core("c_ua", yu, 0)
+    mix(0, yu, 0, 2 * CH)
+    rest(0, yu, (2 * CH, CH + 96))
+    core("c_db", yd, 1)
+    mix(1, yd, 1, 2 * CH + 96)
+    got("r_up", yo, 0)
+    fwd_core("c_oa", yo, 0)
+    got("r_dn", yo, 1)
+    fwd_core("c_ob", yo, 1)
+    rest(1, yd, (CH, 2 * CH + 96))
     transpose_pair(1, ups, put_up)
-    got("c_oa", yo, p0)
-    got("c_ob", yo, p0 + 1)
-    head(yo, 0, CH)
+    core("c_oa", yo, 0)
+    core("c_ob", yo, 1)
+    mix(0, yo, 0, 0, [(1, 0), (1, 512)])
+    mix(0, yo, 1, 96, [(2, 0), (2, 512)])
+    rest(0, yo, (0, 96))
     transpose_pair(0, ups, put_up)
 
     def grad_x(off):
@@ -577,65 +580,65 @@
 
     grad_z(4)
     Z1.first(0)
-    grad_z(3)
-    Z1.go(0, 1, 1, 1)
-    grad_z(-3)
-    Z1.go(0, -1, 0, 1)
+    Z1.first(1)
     for lo in (0, 512):
         dact(0, lo)
     grad_x(2)
     X1.first(0)
-    Z1.first(1)
+    grad_z(3)
+    Z1.go(0, 1, 1, 1)
+    Z1.go(1, 1, 1, 1)
+    grad_z(-3)
+    Z1.go(0, -1, 0, 1)
+    Z1.go(1, -1, 0, 1)
     loss_step(0)
     grad_x(-1)
     X1.go(0, -1, 0, 1)
     grad_x(1)
     X1.go(0, 1, 1, 1)
     Z1.far(0, 2)
-    loss_step(1)
     grad_z(2)
     grad_z(-2)
-    Z1.go(1, 1, 1, 1)
-    Z1.go(1, -1, 0, 1)
-    Z1.near(0, 2)
-    X1.far(0, 2)
+    Z1.far(1, 2)
     grad_z(1)
     grad_z(-1)
     X1.first(1)
-    loss_step(2)
-    Z1.far(0, 3)
+    Z1.near(0, 2)
+    X1.far(0, 2)
     grad_z(0)
     grad_x(0)
-    Z1.far(1, 2)
+    Z1.near(1, 2)
+    loss_step(1)
     X1.go(1, 1, 1, 1)
     X1.go(1, -1, 0, 1)
+    Z1.far(0, 3)
+    Z1.far(1, 3)
+    loss_step(2)
     Z1.near(0, 3)
+    finish_x(0)
+    Z1.near(1, 3)
     loss_step(3)
-    Z1.near(1, 2)
+    X1.far(1, 2)
     Z1.far(0, 4)
-    finish_x(0)
-    X1.far(1, 2)
+    hop(0, 2)
+    Z1.far(1, 4)
     loss_step(4)
-    Z1.far(1, 3)
-    hop(0, 2)
+    hop(0, 3)
+    finish_x(1)
     finish_z(0)
-    Z1.near(1, 3)
     loss_step(5)
-    hop(0, 3)
-    Z1.far(1, 4)
-    finish_x(1)
     hop(0, 4)
+    hop(1, 2)
+    finish_z(1)
     loss_step(6)
     v = loss_z[0]
     for i in range(1, NZ):
         v = v + loss_z[i]
     loss_v[...] = v * (1.0 / (SURV * 2))
     store("loss", loss_v, out_loss)
-    hop(1, 2)
     done_x(0)
+    hop(1, 3)
     done_z(0)
-    finish_z(1)
-    hop(1, 3)
     hop(1, 4)
     done_z(1)
     done_x(1)
@@ -661,7 +664,7 @@
     vmem = pl.BlockSpec(memory_space=pltpu.VMEM)
     hbm = pl.BlockSpec(memory_space=pl.ANY)
     V = pltpu.VMEM
-    piece = (CH, 384)
+    piece = (CH // 2, 768)
     scratch = [
         V((1, SURV), I32), V((1, SURV), I32),
         V((SLOTS, 64, 128), BF16), V((SLOTS, 64, 128), BF16), V((SLOTS, 64, 128), BF16), V((64, D), BF16),
@@ -673,8 +676,8 @@
         V((16, D), F32), V((16, D), F32), V((16, D), F32), V((16, 128), F32), V((16, 128), F32),
         V((ROWS, D), F32), V((ROWS, D), BF16), V((ROWS, HID), BF16), V((ROWS, HID), F32), V((ROWS, HID), BF16),
         V((4, 2, *piece), BF16), V((4, 2, *piece), BF16), V((4, 2, *piece), F32),
-        V((6, *piece), BF16), V((6, *piece), BF16), V((4, 4, *piece), BF16),
-        V((CH, D), F32), V((CH, D), BF16), V((CH, 128), F32), V((ROWS, D), BF16),
+        V((6, *piece), BF16), V((6, *piece), BF16), V((4, 2, 2, *piece), BF16),
+        V((2, CH, D), F32), V((2, CH, D), BF16), V((2, CH, 128), F32), V((ROWS, D), BF16),
         V((NX, 384, ROWS), BF16), V((NZ, 192, ROWS), BF16),
         V((NZ, 4, 192, 256), BF16), V((NX, 4, 384, 256), BF16), V((28, 192, 256), BF16), V((12, 384, 256), BF16),
         V((2, NX, 48, 512), BF16), V((NZ, 4, 48, 256), BF16), V((2, NX, 48, 512), BF16), V((28, 48, 256), BF16),

time: 107 us -> 103 us (0.963)
  Pallas kernels: 101 us -> 97 us
    pallas_call x1, Pallas kernels: 101 us -> 97 us  [shards(): pl.pallas_call(kernel, out_shape=(jax.ShapeDtypeStruct((48, HID), F32), j...]
where the time goes in v3:
time: 103 us
  Pallas kernels  97 us (94%)
  local copies, waits for them, and re-layouts  3.23 us (3%)
  between operations  2.4 us (2%)
    pallas_call x1, Pallas kernels, shards(): pl.pallas_call(kernel, out_shape=(jax.ShapeDtypeStruct((48, HID), F32), j...  97 us
    unnamed x2, local copies, waits for them, and re-layouts  3.23 us

profile of v3, /device:TPU:32, one launch (start us, length us, event | category | flops | bytes accessed | tf_op | source)
XLA Modules:
  0.0 102.6 jit_solution(2595321735746271857)
XLA Ops:
  0.6 97.0 %shard_map.148 = (f32[48,1024]{1,0:T(8,128)}, f32[48,1024]{1,0:T(8,128)}, f32[1,128]{1,0:T(1,128)}) custom-call(s32[192]{0:T(256)} %slot_s.1, s32[192]{0:T(256)} %src_s.1, s32[48]{0:T(128)} %cnt_s.1, s32[1,12]{1,0:T(1,128)} %bitcast.29, s32[2,12]{1,0:T(2,128)} %bitcast.28, s32[1,192]{1,0:T(1,128)} %bitcast.27, s32[1,192]{1,0:T(1,128)} %bitcast.26, ...), custom_call_target="tpu_custom_call" | custom-call | tf_op jit(solution)/shard_map/pallas_call | solution.py:688
  97.6 1.6 %copy.22 = f32[48,1024]{1,0:T(8,128)} copy(f32[48,1024]{1,0:T(8,128)} %get-tuple-element.12) | data formatting | bytes 393216
  99.2 1.6 %copy.23 = f32[48,1024]{1,0:T(8,128)} copy(f32[48,1024]{1,0:T(8,128)} %get-tuple-element.13) | data formatting | bytes 393216

commit v4 on v3

--- a/solution.py
+++ b/solution.py
@@ -24,7 +24,7 @@
 
 def kernel(
     slot_s, src_s, cnt_s, rank_v, time_v, src_h, slot_h, lat_h, noi_h, old_h, wpatch_h, modl_h, wv_h, wup_h, wdn_h,
-    out_up, out_dn, out_loss,
+    out, out_loss,
     src_v, slot_v, lat, noi, old, wpatch, modl, wv, dfin_s, wdn_t, meta, wup, wdn, snd_a, snd_b, rcv_a, rcv_b, meta_l, meta_all, meta_flat, tmp, xs, nz, od,
     mod_s, mod_c, mod_g, coef_u, adv_u, emb, modb, act, dg, dpre, dsend, drecv, pk, ysend, yrecv, pfull,
     fin, finb, inv, ups, mod_t, up_t, gu, gd, zr, xr, s2u, s2d, s2ur, s2dr, loss_own, loss_x, loss_z,
@@ -266,9 +266,6 @@
                 mod_t[xx, (2 * b + zz) * 48 : (2 * b + zz) * 48 + 48, tok] = t[o : o + 48]
 
     presum(3)
-    for p in range(2):
-        transpose_pair(p, modb, put_mod)
-
     part = lambda k, h: pfull.at[k, c, h]
     recv("y2a", yrecv.at[2])
     recv("y3a", yrecv.at[5])
@@ -360,11 +357,21 @@
                 u = 2 * i + step
                 dst[u // 3, (u % 3) * 32 : (u % 3) * 32 + 32, :] = v
 
+    meta_step(4)
+
+    def bounds(g, carry):
+        end = carry[0] + cnt_s[g]
+        out = [end]
+        for i in range(TRAJ):
+            hit = (lead + i >= carry[0]) & (lead + i < end)
+            out += [jnp.where(hit, carry[0], carry[1 + 2 * i]), jnp.where(hit, end, carry[2 + 2 * i])]
+        return tuple(out)
+
+    ends = lax.fori_loop(0, 48, bounds, (jnp.int32(0),) * (1 + 2 * TRAJ))
     recv("c_own", pfull.at[y, 1 - c])
     own = (3 * CH, 3 * CH + 96)
     for t in range(2):
         mix(0, y, t, own[t])
-    meta_step(4)
     meta_step(5)
     meta_sent()
     for r in range(NZ * NX):
@@ -383,15 +390,6 @@
     sq_hi, sq_lo = (sq_i >> 10).astype(F32), (sq_i & 1023).astype(F32)
     jdx = lax.broadcasted_iota(I32, (1, SURV), 1)
 
-    def bounds(g, carry):
-        end = carry[0] + cnt_s[g]
-        out = [end]
-        for i in range(TRAJ):
-            hit = (lead + i >= carry[0]) & (lead + i < end)
-            out += [jnp.where(hit, carry[0], carry[1 + 2 * i]), jnp.where(hit, end, carry[2 + 2 * i])]
-        return tuple(out)
-
-    ends = lax.fori_loop(0, 48, bounds, (jnp.int32(0),) * (1 + 2 * TRAJ))
     for i in range(TRAJ):
         lo_i, hi_i = ends[1 + 2 * i], ends[2 + 2 * i]
         inside = (jdx >= lo_i) & (jdx < hi_i)
@@ -409,13 +407,16 @@
         a = (r - s1 / n) / jnp.maximum(dev_i, 1.0)
         adv_u[2 * i : 2 * i + 2, :] = jnp.broadcast_to(a, (2, 128))
 
-    rest(0, y, own)
     got("g_up_a", yd, 0)
     send("r_up", part(yd, 0), part(yd, 0), dev(dy=1))
     fwd_core("c_da", yd, 0)
     got("g_dn_b", yu, 1)
     send("r_dn", part(yu, 1), part(yu, 1), dev(dy=-1))
     fwd_core("c_ub", yu, 1)
+    rest(0, y, own)
+    for p in range(2):
+        transpose_pair(p, modb, put_mod)
+
     core("c_da", yd, 0)
     core("c_ub", yu, 1)
     mix(0, yu, 1, CH + 96, [(3, 0)])
@@ -442,17 +443,15 @@
     rest(0, yo, (0, 96))
     transpose_pair(0, ups, put_up)
 
-    def grad_x(off):
+    def grad_x(off, b):
         k = at(x, NX, off)
-        for h in range(2):
-            v = jnp.dot(mod_t[k], dpre[:, 512 * h : 512 * h + 512], preferred_element_type=F32).astype(BF16)
-            gd[k, 2 * h], gd[k, 2 * h + 1] = v[:, :256], v[:, 256:]
-
-    def grad_z(off):
+        v = jnp.dot(mod_t[k], dpre[:, 512 * b : 512 * b + 512], preferred_element_type=F32).astype(BF16)
+        gd[k, 2 * b], gd[k, 2 * b + 1] = v[:, :256], v[:, 256:]
+
+    def grad_z(off, b):
         k = at(z, NZ, off)
-        for h in range(2):
-            v = jnp.dot(up_t[k], act[:, 512 * h : 512 * h + 512], preferred_element_type=F32).astype(BF16)
-            gu[k, 2 * h], gu[k, 2 * h + 1] = v[:, :256], v[:, 256:]
+        v = jnp.dot(up_t[k], act[:, 512 * b : 512 * b + 512], preferred_element_type=F32).astype(BF16)
+        gu[k, 2 * b], gu[k, 2 * b + 1] = v[:, :256], v[:, 256:]
 
     def at(axis_pos, n, off):
         return lax.rem(axis_pos + (off + n), n)
@@ -535,7 +534,7 @@
     def done_x(b):
         for h in range(2):
             up_v[b, :, 256 * h : 256 * h + 256] = X2.total(b, h)
-        store(f"up{b}", up_v.at[b], out_up.at[:, pl.ds(512 * b, 512)])
+        store(f"up{b}", up_v.at[b], out.at[0, :, pl.ds(512 * b, 512)])
 
     def finish_z(b):
         for h in range(2):
@@ -551,7 +550,7 @@
             recv(f"t{b}{i}", s2ur.at[b, i])
             v = v + s2ur[b, i].astype(F32)
         dn_v[b] = v
-        store(f"dn{b}", dn_v.at[b], out_dn.at[:, pl.ds(512 * b, 512)])
+        store(f"dn{b}", dn_v.at[b], out.at[1, :, pl.ds(512 * b, 512)])
 
     stores = []
 
@@ -578,66 +577,78 @@
                 if n < 5 or (n == 5 and d == 1):
                     send(f"loss_z{d}_{n}", loss_z.at[(d * (n - 2)) % NZ], loss_z.at[(d * (n - 1)) % NZ], dev(dz=d))
 
-    grad_z(4)
+    grad_z(4, 0)
     Z1.first(0)
+    dact(0, 0)
+    grad_x(2, 0)
+    X1.first(0)
+    grad_z(4, 1)
     Z1.first(1)
-    for lo in (0, 512):
-        dact(0, lo)
-    grad_x(2)
-    X1.first(0)
-    grad_z(3)
+    grad_z(3, 0)
     Z1.go(0, 1, 1, 1)
+    grad_z(-3, 0)
+    Z1.go(0, -1, 0, 1)
+    dact(0, 512)
+    grad_x(-1, 0)
+    X1.go(0, -1, 0, 1)
+    grad_x(1, 0)
+    X1.go(0, 1, 1, 1)
+    loss_step(0)
+    Z1.far(0, 2)
+    grad_z(3, 1)
     Z1.go(1, 1, 1, 1)
-    grad_z(-3)
-    Z1.go(0, -1, 0, 1)
+    grad_z(-3, 1)
     Z1.go(1, -1, 0, 1)
-    loss_step(0)
-    grad_x(-1)
-    X1.go(0, -1, 0, 1)
-    grad_x(1)
-    X1.go(0, 1, 1, 1)
-    Z1.far(0, 2)
-    grad_z(2)
-    grad_z(-2)
+    grad_z(2, 0)
+    grad_z(-2, 0)
     Z1.far(1, 2)
-    grad_z(1)
-    grad_z(-1)
-    X1.first(1)
+    grad_z(2, 1)
+    grad_z(-2, 1)
     Z1.near(0, 2)
     X1.far(0, 2)
-    grad_z(0)
-    grad_x(0)
+    grad_x(2, 1)
+    grad_z(1, 0)
+    grad_z(-1, 0)
+    grad_z(0, 0)
+    grad_x(0, 0)
     Z1.near(1, 2)
     loss_step(1)
-    X1.go(1, 1, 1, 1)
-    X1.go(1, -1, 0, 1)
     Z1.far(0, 3)
+    X1.first(1)
+    grad_x(-1, 1)
+    grad_x(1, 1)
+    grad_z(1, 1)
+    grad_z(-1, 1)
     Z1.far(1, 3)
     loss_step(2)
     Z1.near(0, 3)
+    X1.go(1, 1, 1, 1)
+    X1.go(1, -1, 0, 1)
     finish_x(0)
+    grad_z(0, 1)
+    grad_x(0, 1)
+    X1.far(1, 2)
     Z1.near(1, 3)
     loss_step(3)
-    X1.far(1, 2)
     Z1.far(0, 4)
     hop(0, 2)
     Z1.far(1, 4)
     loss_step(4)
+    finish_x(1)
     hop(0, 3)
-    finish_x(1)
     finish_z(0)
     loss_step(5)
+    hop(1, 2)
     hop(0, 4)
-    hop(1, 2)
-    finish_z(1)
     loss_step(6)
     v = loss_z[0]
     for i in range(1, NZ):
         v = v + loss_z[i]
     loss_v[...] = v * (1.0 / (SURV * 2))
     store("loss", loss_v, out_loss)
+    hop(1, 3)
+    finish_z(1)
     done_x(0)
-    hop(1, 3)
     done_z(0)
     hop(1, 4)
     done_z(1)
@@ -685,15 +696,14 @@
         V((2, 48, 512), F32), V((2, 48, 512), F32), V((1, 128), F32),
         pltpu.SemaphoreType.DMA((10,)), pltpu.SemaphoreType.DMA((5,)), pltpu.SemaphoreType.DMA((NSEM,)), pltpu.SemaphoreType.DMA((NSEM,)),
     ]
-    up, dn, loss = pl.pallas_call(
+    grads, loss = pl.pallas_call(
         kernel,
         out_shape=(
-            jax.ShapeDtypeStruct((48, HID), F32),
-            jax.ShapeDtypeStruct((48, HID), F32),
+            jax.ShapeDtypeStruct((2, 48, HID), F32),
             jax.ShapeDtypeStruct((1, 128), F32),
         ),
         in_specs=[smem] * 3 + [vmem] * 2 + [hbm] * 10,
-        out_specs=(hbm,) * 3,
+        out_specs=(hbm,) * 2,
         scratch_shapes=scratch,
         compiler_params=pltpu.CompilerParams(collective_id=0, has_side_effects=True, vmem_limit_bytes=67043328),
     )(
@@ -703,7 +713,7 @@
         patch_input_weight, modulation_lookup, velocity_head_weight.T,
         up_projection_weight, down_projection_weight,
     )
-    return up, dn, loss[0, 0]
+    return grads[0], grads[1], loss[0, 0]
 
 
 def solution(mesh):

time: 103 us -> 99.3 us (0.964)
  Pallas kernels: 97 us -> 93.6 us
  local copies, waits for them, and re-layouts: 3.23 us -> 1.79 us
    pallas_call x1, Pallas kernels: 97 us -> 93.6 us  [shards(): pl.pallas_call(kernel, out_shape=(jax.ShapeDtypeStruct((2, 48, HID), F32)...]
    unnamed x2 -> x0, local copies, waits for them, and re-layouts: 3.23 us -> none
    squeeze x0 -> x1, local copies, waits for them, and re-layouts: none -> 1.79 us  [shards(): return (grads[0], grads[1], loss[0, 0])]
where the time goes in v4:
time: 99.3 us; the launch traced here: 97.9 us
  Pallas kernels  93.6 us (94%)
  between operations  2.46 us (2%)
  local copies, waits for them, and re-layouts  1.79 us (2%)
    pallas_call x1, Pallas kernels, shards(): pl.pallas_call(kernel, out_shape=(jax.ShapeDtypeStruct((2, 48, HID), F32)...  93.6 us

profile of v4, /device:TPU:32, one launch (start us, length us, event | category | flops | bytes accessed | tf_op | source)
XLA Modules:
  0.0 97.9 jit_solution(3984947879430120556)
XLA Ops:
  0.6 93.6 %shard_map.148 = (f32[2,48,1024]{2,1,0:T(8,128)}, f32[1,128]{1,0:T(1,128)}) custom-call(s32[192]{0:T(256)} %slot_s.1, s32[192]{0:T(256)} %src_s.1, s32[48]{0:T(128)} %cnt_s.1, s32[1,12]{1,0:T(1,128)} %bitcast.33, s32[2,12]{1,0:T(2,128)} %bitcast.32, s32[1,192]{1,0:T(1,128)} %bitcast.31, s32[1,192]{1,0:T(1,128)} %bitcast.30, bf16[12,64,128]{2,1,0:T(8,128)(2,1)} %bitcast.26, ...), custom_call_target="tpu_custom_call" | custom-call | tf_op jit(solution)/shard_map/pallas_call | solution.py:699
  94.3 1.8 %slice_bitcast_fusion = (f32[48,1024]{1,0:T(8,128)}, f32[48,1024]{1,0:T(8,128)}) fusion(f32[2,48,1024]{2,1,0:T(8,128)} %get-tuple-element.5), kind=kLoop, calls=%fused_computation | loop fusion | bytes 786432 | tf_op jit(solution)/shard_map/squeeze | solution.py:716

commit v5 on v4

--- a/solution.py
+++ b/solution.py
@@ -194,11 +194,18 @@
     def up(s, n):
         rows, cols = slice(s * CH, s * CH + CH), slice(256 * n, 256 * n + 256)
         pre = jnp.dot(modb[rows, :], wup[:, cols], preferred_element_type=F32)
-        sq = pre * pre
-        th = jnp.tanh(GELU_K * (pre + GELU_C * (sq * pre)))
-        half = 0.5 * (1.0 + th)
-        act[rows, cols] = (pre * half).astype(BF16)
-        dg[rows, cols] = half + (0.5 * GELU_K) * pre * (1.0 - th * th) * (1.0 + 3.0 * GELU_C * sq)
+        th = jnp.tanh(GELU_K * (pre + GELU_C * (pre * pre * pre)))
+        act[rows, cols] = (pre * (0.5 * (1.0 + th))).astype(BF16)
+        dg[rows, cols] = pre
+
+    def slope_of(s):
+        rows = slice(s * CH, s * CH + CH)
+        for n in range(4):
+            cols = slice(256 * n, 256 * n + 256)
+            pre = dg[rows, cols]
+            sq = pre * pre
+            th = jnp.tanh(GELU_K * (pre + GELU_C * (sq * pre)))
+            dg[rows, cols] = 0.5 * (1.0 + th) + (0.5 * GELU_K) * pre * (1.0 - th * th) * (1.0 + 3.0 * GELU_C * sq)
 
     def down(s):
         rows = slice(s * CH, s * CH + CH)
@@ -407,6 +414,7 @@
         a = (r - s1 / n) / jnp.maximum(dev_i, 1.0)
         adv_u[2 * i : 2 * i + 2, :] = jnp.broadcast_to(a, (2, 128))
 
+    slope_of(0)
     got("g_up_a", yd, 0)
     send("r_up", part(yd, 0), part(yd, 0), dev(dy=1))
     fwd_core("c_da", yd, 0)
@@ -414,6 +422,7 @@
     send("r_dn", part(yu, 1), part(yu, 1), dev(dy=-1))
     fwd_core("c_ub", yu, 1)
     rest(0, y, own)
+    slope_of(3)
     for p in range(2):
         transpose_pair(p, modb, put_mod)
 
@@ -425,6 +434,8 @@
     fwd_core("c_ua", yu, 0)
     got("g_up_b", yd, 1)
     fwd_core("c_db", yd, 1)
+    slope_of(1)
+    slope_of(2)
     core("c_ua", yu, 0)
     mix(0, yu, 0, 2 * CH)
     rest(0, yu, (2 * CH, CH + 96))
@@ -632,27 +643,27 @@
     loss_step(3)
     Z1.far(0, 4)
     hop(0, 2)
+    finish_x(1)
     Z1.far(1, 4)
     loss_step(4)
-    finish_x(1)
     hop(0, 3)
+    hop(1, 2)
     finish_z(0)
     loss_step(5)
-    hop(1, 2)
     hop(0, 4)
+    hop(1, 3)
+    finish_z(1)
     loss_step(6)
     v = loss_z[0]
     for i in range(1, NZ):
         v = v + loss_z[i]
     loss_v[...] = v * (1.0 / (SURV * 2))
     store("loss", loss_v, out_loss)
-    hop(1, 3)
-    finish_z(1)
+    hop(1, 4)
     done_x(0)
     done_z(0)
-    hop(1, 4)
+    done_x(1)
     done_z(1)
-    done_x(1)
     for d in stores:
         d.wait()
     for d in sent:

time: 99.3 us -> 97.7 us (0.984); the launches traced: 97.9 us -> 97.6 us
  no operation moved by 1% of the time
where the time goes in v5:
time: 97.7 us; the launch traced here: 97.6 us
  Pallas kernels  93.3 us (95%)
  between operations  2.46 us (3%)
  local copies, waits for them, and re-layouts  1.79 us (2%)
    pallas_call x1, Pallas kernels, shards(): pl.pallas_call(kernel, out_shape=(jax.ShapeDtypeStruct((2, 48, HID), F32)...  93.3 us

profile of v5, /device:TPU:32, one launch (start us, length us, event | category | flops | bytes accessed | tf_op | source)
XLA Modules:
  0.0 97.6 jit_solution(814802668520334929)
XLA Ops:
  0.6 93.3 %shard_map.148 = (f32[2,48,1024]{2,1,0:T(8,128)}, f32[1,128]{1,0:T(1,128)}) custom-call(s32[192]{0:T(256)} %slot_s.1, s32[192]{0:T(256)} %src_s.1, s32[48]{0:T(128)} %cnt_s.1, s32[1,12]{1,0:T(1,128)} %bitcast.33, s32[2,12]{1,0:T(2,128)} %bitcast.32, s32[1,192]{1,0:T(1,128)} %bitcast.31, s32[1,192]{1,0:T(1,128)} %bitcast.30, bf16[12,64,128]{2,1,0:T(8,128)(2,1)} %bitcast.26, ...), custom_call_target="tpu_custom_call" | custom-call | tf_op jit(solution)/shard_map/pallas_call | solution.py:710
  94.0 1.8 %slice_bitcast_fusion = (f32[48,1024]{1,0:T(8,128)}, f32[48,1024]{1,0:T(8,128)}) fusion(f32[2,48,1024]{2,1,0:T(8,128)} %get-tuple-element.5), kind=kLoop, calls=%fused_computation | loop fusion | bytes 786432 | tf_op jit(solution)/shard_map/squeeze | solution.py:727

commit v6 on v5

--- a/solution.py
+++ b/solution.py
@@ -449,8 +449,8 @@
     transpose_pair(1, ups, put_up)
     core("c_oa", yo, 0)
     core("c_ob", yo, 1)
-    mix(0, yo, 0, 0, [(1, 0), (1, 512)])
-    mix(0, yo, 1, 96, [(2, 0), (2, 512)])
+    mix(0, yo, 0, 0, [(1, 0)])
+    mix(0, yo, 1, 96, [(2, 0)])
     rest(0, yo, (0, 96))
     transpose_pair(0, ups, put_up)
 
@@ -599,7 +599,6 @@
     Z1.go(0, 1, 1, 1)
     grad_z(-3, 0)
     Z1.go(0, -1, 0, 1)
-    dact(0, 512)
     grad_x(-1, 0)
     X1.go(0, -1, 0, 1)
     grad_x(1, 0)
@@ -617,6 +616,8 @@
     grad_z(-2, 1)
     Z1.near(0, 2)
     X1.far(0, 2)
+    for slot in range(3):
+        dact(slot * CH, 512)
     grad_x(2, 1)
     grad_z(1, 0)
     grad_z(-1, 0)

time: 97.7 us -> 97.1 us (level)
  no operation moved by 1% of the time
where the time goes in v6:
time: 97.1 us; the launch traced here: 97 us
  Pallas kernels  92.7 us (95%)
  between operations  2.46 us (3%)
  local copies, waits for them, and re-layouts  1.79 us (2%)
    pallas_call x1, Pallas kernels, shards(): pl.pallas_call(kernel, out_shape=(jax.ShapeDtypeStruct((2, 48, HID), F32)...  92.7 us

profile of v6, /device:TPU:32, one launch (start us, length us, event | category | flops | bytes accessed | tf_op | source)
XLA Modules:
  0.0 97.0 jit_solution(2548421883031603463)
XLA Ops:
  0.6 92.7 %shard_map.148 = (f32[2,48,1024]{2,1,0:T(8,128)}, f32[1,128]{1,0:T(1,128)}) custom-call(s32[192]{0:T(256)} %slot_s.1, s32[192]{0:T(256)} %src_s.1, s32[48]{0:T(128)} %cnt_s.1, s32[1,12]{1,0:T(1,128)} %bitcast.33, s32[2,12]{1,0:T(2,128)} %bitcast.32, s32[1,192]{1,0:T(1,128)} %bitcast.31, s32[1,192]{1,0:T(1,128)} %bitcast.30, bf16[12,64,128]{2,1,0:T(8,128)(2,1)} %bitcast.26, ...), custom_call_target="tpu_custom_call" | custom-call | tf_op jit(solution)/shard_map/pallas_call | solution.py:711
  93.3 1.8 %slice_bitcast_fusion = (f32[48,1024]{1,0:T(8,128)}, f32[48,1024]{1,0:T(8,128)}) fusion(f32[2,48,1024]{2,1,0:T(8,128)} %get-tuple-element.5), kind=kLoop, calls=%fused_computation | loop fusion | bytes 786432 | tf_op jit(solution)/shard_map/squeeze | solution.py:728
